TPU v7x, 8 devices: a whole 2x2x1 slice. The times are simulated.
8 devices in a mesh: rep: 2 (over y, z), dp: 4 (over x, core).
Axes of the slice: x: 2, y: 2, z: 1, core: 2. Of those that a mesh axis runs over, the one named last changes fastest.
Arguments:
- x: bfloat16 [8, 2048, 768], P(('rep', 'dp')), parts along dimension 0
- dy: bfloat16 [8, 2048, 768], P(('rep', 'dp')), parts along dimension 0
- w_gate: bfloat16 [2, 768, 3072], P(None, 'dp')
- w_up: bfloat16 [2, 768, 3072], P(None, 'dp')
- w_down: bfloat16 [2, 3072, 768], P(None, 'dp')
- m_w_gate: float32 [2, 768, 3072], P(None, 'dp')
- m_w_up: float32 [2, 768, 3072], P(None, 'dp')
- m_w_down: float32 [2, 3072, 768], P(None, 'dp')
- v_w_gate: float32 [2, 768, 3072], P(None, 'dp')
- v_w_up: float32 [2, 768, 3072], P(None, 'dp')
- v_w_down: float32 [2, 3072, 768], P(None, 'dp')
Outputs:
- output 1: bfloat16 [4, 768, 3072], P('rep', 'dp'), parts along dimension 0
- output 2: bfloat16 [4, 768, 3072], P('rep', 'dp'), parts along dimension 0
- output 3: bfloat16 [4, 3072, 768], P('rep', 'dp'), parts along dimension 0
- output 4: float32 [4, 768, 3072], P('rep', 'dp'), parts along dimension 0
- output 5: float32 [4, 768, 3072], P('rep', 'dp'), parts along dimension 0
- output 6: float32 [4, 3072, 768], P('rep', 'dp'), parts along dimension 0
- output 7: float32 [4, 768, 3072], P('rep', 'dp'), parts along dimension 0
- output 8: float32 [4, 768, 3072], P('rep', 'dp'), parts along dimension 0
- output 9: float32 [4, 3072, 768], P('rep', 'dp'), parts along dimension 0
There are 2 independent parts. A program takes and returns all parts, laid end to end along the dimension named above; an argument that names none is the same for every part.
All inputs are finite; a program needn't handle non-finite values.
Results may differ from a plain program's by a relative error of at most 0.022.
Values are sent between devices in bfloat16 or wider.
A program may use at most 2 GiB of HBM per device.

v0:
```python
import jax
import jax.numpy as jnp
from jax import lax
from jax.sharding import PartitionSpec as P

NAMES = ("w_gate", "w_up", "w_down")


def matmul(a, w):
    return jnp.dot(a, w, preferred_element_type=jnp.float32).astype(jnp.bfloat16)


def normed(h):
    wide = h.astype(jnp.float32)
    scale = lax.rsqrt(jnp.mean(wide**2, -1, keepdims=True) + 1e-6)
    return (wide * scale).astype(jnp.bfloat16)


def layer(h, w):
    a = normed(h)
    gate = jnp.dot(a, w["w_gate"], preferred_element_type=jnp.float32)
    up = jnp.dot(a, w["w_up"], preferred_element_type=jnp.float32)
    return h + matmul((jax.nn.silu(gate) * up).astype(jnp.bfloat16), w["w_down"])


def adamw(w, m, v, g):
    m = 0.9 * m + 0.1 * g
    v = 0.95 * v + 0.05 * g * g
    step = m * lax.rsqrt(v + 1e-8) + 0.1 * w
    return (w - 0.02 * step).astype(jnp.bfloat16), m, v


def clipped(gradients, sum_of_squares, count):
    factor = jnp.minimum(1.0, 0.5 * lax.rsqrt(sum_of_squares / count + 1e-30))
    return [g * factor for g in gradients]


def solution(mesh):
    def fetched(weights, number):
        return {name: lax.all_gather(w[number], "dp", axis=0, tiled=True) for name, w in zip(NAMES, weights, strict=True)}

    def step(x, dy, *arrays):
        weights, m, v = (arrays[i : i + 3] for i in (0, 3, 6))
        layers = weights[0].shape[0]
        h, kept = x[0], []
        for number in range(layers):
            kept.append(h)
            h = layer(h, fetched(weights, number))
        by_h, mine = dy[0], [None] * layers
        for number in reversed(range(layers)):
            _, back = jax.vjp(lambda w, h: layer(h, w), fetched(weights, number), kept[number])
            by_w, by_h = back(by_h)
            mine[number] = [lax.psum_scatter(by_w[name], "dp", scatter_dimension=0, tiled=True) for name in NAMES]
        gradients = [jnp.stack([mine[number][i] for number in range(layers)]).astype(jnp.float32) for i in range(3)]
        squares = lax.psum(sum(jnp.sum(g * g) for g in gradients), "dp")
        gradients = clipped(gradients, squares, lax.psum(1, "dp") * sum(g.size for g in gradients))
        new = [adamw(w.astype(jnp.float32), m, v, g) for w, m, v, g in zip(weights, m, v, gradients, strict=True)]
        return tuple(one[which] for which in range(3) for one in new)

    states, cut = P(("rep", "dp"), None, None), P(None, "dp", None)
    return jax.shard_map(
        step,
        mesh=mesh,
        in_specs=(states, states) + (cut,) * 9,
        out_specs=(P("rep", "dp", None),) * 9,
        check_vma=False,
    )
```

profile of v0, /device:TPU:0, one launch (start us, length us, event | category | flops | bytes accessed | tf_op | source)
XLA Modules:
  0.0 630.4 jit_solution(16480182095320210521)
XLA Ops:
  7.2 3.2 fusion.104
  10.4 0.0 all-gather.15.cloned.1.call-start
  10.5 3.3 fusion.103
  13.9 1.6 fusion.102
  15.5 0.5 all-gather.21.cloned.1.call-update
  16.1 0.5 all-gather.23.cloned.1.call-update
  16.7 0.5 all-gather.19.cloned.1.call-update
  17.3 3.2 copy.20
  20.5 0.7 fusion.15
  21.2 5.0 copy.21
  26.2 21.8 %all-gather.13.cloned.1.call-done = bf16[1,768,3072]{2,1,0:T(8,128)(2,1)} async-done(((bf16[1,192,3072]{2,1,0:T(8,128)(2,1)}), bf16[1,768,3072]{2,1,0:T(8,128)(2,1)}) %all-gather.13.cloned.1.call-update) | async-done | bytes 4718608 | tf_op jit(solution)/shard_map/all_gather | solution.py:40
  47.9 15.7 %fusion.62 = f32[2048,3072]{1,0:T(8,128)} fusion(bf16[1,768,3072]{2,1,0:T(8,128)(2,1)} %all-gather.13.cloned.1.call-done, bf16[1,2048,768]{1,2,0:T(8,128)(2,1)S(1)} %copy.20, f32[2048]{0:T(1024)S(1)} %add_rsqrt_fusion), kind=kOutput, calls=%fused_computation.95 | convolution fusion | flops 9668395008 | bytes 33038336 | tf_op jit(solution)/shard_map/dot_general | solution.py:21
  63.7 20.9 %all-gather.15.cloned.1.call-done = bf16[1,768,3072]{2,1,0:T(8,128)(2,1)} async-done(((bf16[1,192,3072]{2,1,0:T(8,128)(2,1)}), bf16[1,768,3072]{2,1,0:T(8,128)(2,1)}) %all-gather.15.cloned.1.call-update) | async-done | bytes 4718608 | tf_op jit(solution)/shard_map/all_gather | solution.py:40
  84.6 26.0 %multiply_convert_fusion.1 = (bf16[2048,3072]{1,0:T(8,128)(2,1)}, f32[2048,3072]{1,0:T(8,128)}) fusion(f32[2048,3072]{1,0:T(8,128)} %fusion.62, bf16[1,768,3072]{2,1,0:T(8,128)(2,1)} %all-gather.15.cloned.1.call-done, bf16[1,2048,768]{1,2,0:T(8,128)(2,1)S(1)} %copy.20, f32[2048]{0:T(1024)S(1)} %add_rsqrt_fusion), kind=kOutput, calls=%fused_computation.17 | convolution fusion | flops 9706143744 | bytes 70787072 | tf_op jit(solution)/shard_map/dot_general | solution.py:22
  110.7 10.6 %all-gather.17.cloned.1.call-done = bf16[1,3072,768]{2,1,0:T(8,128)(2,1)} async-done(((bf16[1,768,768]{2,1,0:T(8,128)(2,1)}), bf16[1,3072,768]{2,1,0:T(8,128)(2,1)}) %all-gather.17.cloned.1.call-update) | async-done | bytes 4718608 | tf_op jit(solution)/shard_map/all_gather | solution.py:40
  121.3 16.2 %fusion.19 = (f32[2048]{0:T(1024)S(1)}, bf16[2048,768]{0,1:T(8,128)(2,1)}) fusion(bf16[2048,3072]{1,0:T(8,128)(2,1)} %get-tuple-element.24, bf16[1,3072,768]{2,1,0:T(8,128)(2,1)} %all-gather.17.cloned.1.call-done, bf16[1,2048,768]{1,2,0:T(8,128)(2,1)S(1)} %copy.20), kind=kOutput, calls=%fused_computation.40 | convolution fusion | flops 9671538688 | bytes 23601152 | tf_op jit(solution)/shard_map/dot_general | solution.py:10
  137.4 0.6 copy-done.18
  138.1 19.8 %all-gather.21.cloned.1.call-done = bf16[1,3072,768]{2,1,0:T(8,128)(2,1)} async-done(((bf16[1,768,768]{2,1,0:T(8,128)(2,1)}), bf16[1,3072,768]{2,1,0:T(8,128)(2,1)}) %all-gather.21.cloned.1.call-update) | async-done | bytes 4718608 | tf_op jit(solution)/shard_map/all_gather | solution.py:40
  157.8 15.7 %convolution_convert_fusion.1 = bf16[2048,3072]{1,0:T(8,128)(2,1)} fusion(bf16[1,3072,768]{2,1,0:T(8,128)(2,1)} %all-gather.21.cloned.1.call-done, bf16[1,2048,768]{2,1,0:T(8,128)(2,1)} %param.12), kind=kOutput, calls=%fused_computation.25 | convolution fusion | flops 9669967872 | bytes 20447232 | tf_op jit(solution)/shard_map/transpose(jvp())/dot_general | solution.py:10
  173.5 20.8 %all-gather.23.cloned.1.call-done = bf16[1,768,3072]{2,1,0:T(8,128)(2,1)} async-done(((bf16[1,192,3072]{2,1,0:T(8,128)(2,1)}), bf16[1,768,3072]{2,1,0:T(8,128)(2,1)}) %all-gather.23.cloned.1.call-update) | async-done | bytes 4718608 | tf_op jit(solution)/shard_map/all_gather | solution.py:40
  194.3 15.8 %fusion.49 = f32[2048,3072]{1,0:T(8,128)} fusion(bf16[1,768,3072]{2,1,0:T(8,128)(2,1)} %all-gather.23.cloned.1.call-done, bf16[2048,768]{0,1:T(8,128)(2,1)S(1)} %copy-done.13, f32[2048]{0:T(1024)S(1)} %fusion.90), kind=kOutput, calls=%fused_computation.82 | convolution fusion | flops 9668395008 | bytes 33038336 | tf_op jit(solution)/shard_map/jvp()/dot_general | solution.py:22
  210.1 20.7 %all-gather.19.cloned.1.call-done = bf16[1,768,3072]{2,1,0:T(8,128)(2,1)} async-done(((bf16[1,192,3072]{2,1,0:T(8,128)(2,1)}), bf16[1,768,3072]{2,1,0:T(8,128)(2,1)}) %all-gather.19.cloned.1.call-update) | async-done | bytes 4718608 | tf_op jit(solution)/shard_map/all_gather | solution.py:40
  230.8 33.1 %fusion.2 = (bf16[2048,3072]{1,0:T(8,128)(2,1)}, f32[2048,3072]{1,0:T(8,128)}) fusion(f32[2048,3072]{1,0:T(8,128)} %fusion.49, bf16[2048,3072]{1,0:T(8,128)(2,1)} %convolution_convert_fusion.1, bf16[1,768,3072]{2,1,0:T(8,128)(2,1)} %all-gather.19.cloned.1.call-done, bf16[2048,768]{0,1:T(8,128)(2,1)S(1)} %copy-done.13, f32[2048]{0:T(1024)S(1)} %fusion.90), kind=kOutput, calls=%fused_computation.8 | convolution fusion | flops 9743892480 | bytes 83369984 | tf_op jit(solution)/shard_map/jvp()/dot_general | solution.py:21
  264.0 19.6 %fusion.65 = bf16[2048,768]{0,1:T(8,128)(2,1)} fusion(bf16[1,768,3072]{2,1,0:T(8,128)(2,1)} %all-gather.23.cloned.1.call-done, bf16[2048,3072]{1,0:T(8,128)(2,1)} %convolution_convert_fusion.1, f32[2048,3072]{1,0:T(8,128)} %get-tuple-element.29), kind=kOutput, calls=%fused_computation.97 | convolution fusion | flops 9702998016 | bytes 45613056 | tf_op jit(solution)/shard_map/transpose(jvp())/dot_general | solution.py:22
  283.6 15.8 %fusion.21 = (f32[2048]{0:T(1024)S(1)}, bf16[2048,768]{0,1:T(8,128)(2,1)S(1)}) fusion(bf16[2048,768]{0,1:T(8,128)(2,1)S(1)} %copy-done.13, bf16[2048,768]{0,1:T(8,128)(2,1)} %fusion.65, bf16[2048,3072]{1,0:T(8,128)(2,1)} %get-tuple-element.28, bf16[1,768,3072]{2,1,0:T(8,128)(2,1)} %all-gather.19.cloned.1.call-done), kind=kOutput, calls=%fused_computation.42 | convolution fusion | flops 9671538688 | bytes 26746880 | tf_op jit(solution)/shard_map/transpose(jvp())/dot_general | solution.py:21
  299.5 2.2 fusion.74
  301.7 1.7 copy-done.15
  303.4 14.6 %convolution_convert_fusion.2 = bf16[3072,768]{1,0:T(8,128)(2,1)} fusion(bf16[2048,3072]{1,0:T(8,128)(2,1)} %get-tuple-element.24, bf16[2048,768]{0,1:T(8,128)(2,1)S(1)} %fusion.74), kind=kOutput, calls=%fused_computation.62 | convolution fusion | flops 9666035712 | bytes 20447232 | tf_op jit(solution)/shard_map/transpose(jvp())/dot_general | solution.py:10
  318.0 1.8 copy-done.12
  319.8 22.5 %fusion.25 = bf16[3072,768]{1,0:T(8,128)(2,1)} fusion(f32[2048,3072]{1,0:T(8,128)} %fusion.49, bf16[1,2048,768]{2,1,0:T(8,128)(2,1)S(1)} %copy-done.12, f32[2048,3072]{1,0:T(8,128)} %get-tuple-element.29), kind=kOutput, calls=%fused_computation.58 | convolution fusion | flops 9703784448 | bytes 58195968 | tf_op jit(solution)/shard_map/transpose(jvp())/dot_general | solution.py:10
  342.4 15.8 %convolution_convert_fusion = bf16[2048,3072]{1,0:T(8,128)(2,1)} fusion(bf16[2048,768]{0,1:T(8,128)(2,1)} %copy-done.15, bf16[1,3072,768]{2,1,0:T(8,128)(2,1)} %all-gather.17.cloned.1.call-done), kind=kOutput, calls=%fused_computation.24 | convolution fusion | flops 9669967872 | bytes 20447232 | tf_op jit(solution)/shard_map/transpose(jvp())/dot_general | solution.py:10
  358.3 18.4 %fusion.30 = bf16[768,3072]{1,0:T(8,128)(2,1)} fusion(bf16[2048,3072]{1,0:T(8,128)(2,1)} %convolution_convert_fusion, f32[2048,3072]{1,0:T(8,128)} %fusion.62, bf16[1,2048,768]{1,2,0:T(8,128)(2,1)S(1)} %copy-done.1, f32[2048]{0:T(1024)S(1)} %copy-done.21), kind=kOutput, calls=%fused_computation.61 | convolution fusion | flops 9708503040 | bytes 45621248 | tf_op jit(solution)/shard_map/transpose(jvp())/dot_general | solution.py:22
  376.7 0.6 copy-done.17
  377.3 19.5 %fusion.26 = bf16[768,3072]{1,0:T(8,128)(2,1)} fusion(bf16[2048,3072]{1,0:T(8,128)(2,1)} %convolution_convert_fusion.1, bf16[2048,768]{0,1:T(8,128)(2,1)} %get-tuple-element.27, f32[2048]{0:T(1024)S(1)} %copy-done.17, f32[2048,3072]{1,0:T(8,128)} %get-tuple-element.29), kind=kOutput, calls=%fused_computation.59 | convolution fusion | flops 9708503040 | bytes 45621248 | tf_op jit(solution)/shard_map/transpose(jvp())/dot_general | solution.py:22
  396.9 25.9 %fusion.27 = bf16[768,3072]{1,0:T(8,128)(2,1)} fusion(f32[2048,3072]{1,0:T(8,128)} %fusion.62, f32[2048,3072]{1,0:T(8,128)} %get-tuple-element.25, bf16[2048,3072]{1,0:T(8,128)(2,1)} %convolution_convert_fusion, bf16[1,2048,768]{1,2,0:T(8,128)(2,1)S(1)} %copy-done.1, f32[2048]{0:T(1024)S(1)} %copy-done.21), kind=kOutput, calls=%fused_computation.60 | convolution fusion | flops 9739960320 | bytes 70787072 | tf_op jit(solution)/shard_map/transpose(jvp())/dot_general | solution.py:21
  422.9 1.8 copy-done.14
  424.7 14.5 %convolution_convert_fusion.3 = bf16[768,3072]{1,0:T(8,128)(2,1)} fusion(bf16[2048,3072]{1,0:T(8,128)(2,1)} %get-tuple-element.28, bf16[2048,768]{0,1:T(8,128)(2,1)S(1)} %copy-done.14, f32[2048]{0:T(1024)S(1)} %copy-done.17), kind=kOutput, calls=%fused_computation.63 | convolution fusion | flops 9668395008 | bytes 20455424 | tf_op jit(solution)/shard_map/transpose(jvp())/dot_general | solution.py:21
  439.3 3.6 fusion.39
  442.9 6.1 reduce-scatter.11.cloned.1.call-done
  449.0 44.5 %reduce-scatter.13.cloned.1.call-done = bf16[192,3072]{1,0:T(8,128)(2,1)} async-done(((bf16[768,3072]{1,0:T(8,128)(2,1)}), bf16[192,3072]{1,0:T(8,128)(2,1)}) %reduce-scatter.13.cloned.1.call-update) | async-done | bytes 1179664 | tf_op jit(solution)/shard_map/reduce_scatter | solution.py:53
  493.5 3.4 fusion.38
  497.0 41.2 %reduce-scatter.7.cloned.1.call-done = bf16[192,3072]{1,0:T(8,128)(2,1)} async-done(((bf16[768,3072]{1,0:T(8,128)(2,1)}), bf16[192,3072]{1,0:T(8,128)(2,1)}) %reduce-scatter.7.cloned.1.call-update) | async-done | bytes 1179664 | tf_op jit(solution)/shard_map/reduce_scatter | solution.py:53
  538.2 44.5 %reduce-scatter.9.cloned.1.call-done = bf16[192,3072]{1,0:T(8,128)(2,1)} async-done(((bf16[768,3072]{1,0:T(8,128)(2,1)}), bf16[192,3072]{1,0:T(8,128)(2,1)}) %reduce-scatter.9.cloned.1.call-update) | async-done | bytes 1179664 | tf_op jit(solution)/shard_map/reduce_scatter | solution.py:53
  582.7 3.4 fusion.37
  588.1 6.3 psum.7
  595.2 9.9 %fusion.45 = (bf16[2,768,768]{2,1,0:T(8,128)(2,1)}, f32[2,768,768]{2,1,0:T(8,128)}, f32[2,768,768]{2,1,0:T(8,128)}) fusion(bf16[2,768,768]{2,1,0:T(8,128)(2,1)S(1)} %copy-done.4, f32[]{:T(128)S(6)} %min_shard_map.3, bf16[1,768,768]{2,1,0:T(8,128)(2,1)} %bitcast.75, bf16[1,768,768]{2,1,0:T(8,128)(2,1)S(1)} %bitcast.73, f32[2,768,768]{2,1,0:T(8,128)} %param.21, ...), kind=kLoop, calls=%fused_computation.78 | loop fusion | flops 23592960 | bytes 25952260 | tf_op jit(solution)/shard_map/convert_element_type | solution.py:30
  605.1 0.9 copy-done.11
  606.0 17.2 %fusion.36 = (bf16[2,192,3072]{2,1,0:T(8,128)(2,1)}, f32[2,192,3072]{2,1,0:T(8,128)}, f32[2,192,3072]{2,1,0:T(8,128)}, bf16[2,192,3072]{2,1,0:T(8,128)(2,1)}, f3...) fusion(bf16[2,192,3072]{2,1,0:T(8,128)(2,1)S(1)} %copy-done.5, f32[]{:T(128)S(6)} %min_shard_map.3, ...), kind=kLoop, calls=%fused_computation.69 | loop fusion | flops 47185920 | bytes 51904516 | tf_op jit(solution)/shard_map/convert_element_type | solution.py:30
  (63 shorter events, 0.7 us)
Async XLA Ops:
  7.2 40.8 %all-gather.13.cloned.1.call-start = ((), (), s32[]{:S(2)}) async-start(), calls=%async_computation.12 | async-start | bytes 5898240 | tf_op jit(solution)/shard_map/all_gather | solution.py:40
  10.4 3.5 copy-start.3
  10.4 74.2 %all-gather.15.cloned.1.call-start = ((), (), s32[]{:S(2)}) async-start(), calls=%async_computation.13 | async-start | bytes 5898240 | tf_op jit(solution)/shard_map/all_gather | solution.py:40
  13.8 107.4 %all-gather.17.cloned.1.call-start = ((), (), s32[]{:S(2)}) async-start(), calls=%async_computation.14 | async-start | bytes 5898240 | tf_op jit(solution)/shard_map/all_gather | solution.py:40
  15.5 142.3 %all-gather.21.cloned.1.call-start = ((), (), s32[]{:S(2)}) async-start(), calls=%async_computation.16 | async-start | bytes 5898240 | tf_op jit(solution)/shard_map/all_gather | solution.py:40
  16.1 178.3 %all-gather.23.cloned.1.call-start = ((), (), s32[]{:S(2)}) async-start(), calls=%async_computation.17 | async-start | bytes 5898240 | tf_op jit(solution)/shard_map/all_gather | solution.py:40
  16.6 214.2 %all-gather.19.cloned.1.call-start = ((), (), s32[]{:S(2)}) async-start(), calls=%async_computation.15 | async-start | bytes 5898240 | tf_op jit(solution)/shard_map/all_gather | solution.py:40
  17.2 422.0 %reduce-scatter.15.cloned.1.call-start = ((), (), s32[]{:S(2)}) async-start(), calls=%async_computation.10 | async-start | bytes 5898240 | tf_op jit(solution)/shard_map/reduce_scatter | solution.py:53
  20.5 100.8 %copy-start = (bf16[1,2048,768]{1,2,0:T(8,128)(2,1)}, bf16[1,2048,768]{1,2,0:T(8,128)(2,1)S(1)}, u32[]{:S(2)}) copy-start(bf16[1,2048,768]{1,2,0:T(8,128)(2,1)S(1)} %copy.20) | copy-start | bytes 9437188
  21.2 63.5 %copy-start.20 = (f32[2048]{0:T(1024)}, f32[2048]{0:T(1024)S(1)}, u32[]{:S(2)}) copy-start(f32[2048]{0:T(1024)S(1)} %add_rsqrt_fusion) | copy-start | bytes 24580
  137.4 0.6 copy-start.18
  138.0 161.4 %copy-start.16 = (f32[2048]{0:T(1024)}, f32[2048]{0:T(1024)S(1)}, u32[]{:S(2)}) copy-start(f32[2048]{0:T(1024)S(1)} %fusion.90) | copy-start | bytes 24580
  138.0 56.3 %copy-start.13 = (bf16[2048,768]{0,1:T(8,128)(2,1)S(1)}, bf16[2048,768]{0,1:T(8,128)(2,1)}, u32[]{:S(2)}) copy-start(bf16[2048,768]{0,1:T(8,128)(2,1)} %get-tuple-element.27) | copy-start | bytes 9437188
  283.6 15.8 %copy-start.19 = (f32[2048]{0:T(1024)S(1)}, f32[2048]{0:T(1024)}, u32[]{:S(2)}) copy-start(f32[2048]{0:T(1024)} %copy-done.18) | copy-start | bytes 24580
  283.6 15.9 %copy-start.2 = (bf16[1,2048,768]{1,2,0:T(8,128)(2,1)S(1)}, bf16[1,2048,768]{1,2,0:T(8,128)(2,1)}, u32[]{:S(2)}) copy-start(bf16[1,2048,768]{1,2,0:T(8,128)(2,1)} %copy.21) | copy-start | bytes 9437188
  301.7 1.7 copy-start.15
  317.9 1.9 copy-start.12
  318.0 121.3 %reduce-scatter.17.cloned.1.call-start = ((), (), s32[]{:S(2)}) async-start(), calls=%async_computation.11 | async-start | bytes 5898240 | tf_op jit(solution)/shard_map/reduce_scatter | solution.py:53
  342.4 15.9 %copy-start.1 = (bf16[1,2048,768]{1,2,0:T(8,128)(2,1)S(1)}, bf16[1,2048,768]{1,2,0:T(8,128)(2,1)}, u32[]{:S(2)}) copy-start(bf16[1,2048,768]{1,2,0:T(8,128)(2,1)} %copy-done) | copy-start | bytes 9437188
  342.4 15.9 %copy-start.21 = (f32[2048]{0:T(1024)S(1)}, f32[2048]{0:T(1024)}, u32[]{:S(2)}) copy-start(f32[2048]{0:T(1024)} %copy-done.20) | copy-start | bytes 24580
  342.4 106.6 %reduce-scatter.11.cloned.1.call-start = ((), (), s32[]{:S(2)}) async-start(), calls=%async_computation.8 | async-start | bytes 5898240 | tf_op jit(solution)/shard_map/reduce_scatter | solution.py:53
  376.6 0.7 copy-start.17
  376.7 116.9 %reduce-scatter.13.cloned.1.call-start = ((), (), s32[]{:S(2)}) async-start(), calls=%async_computation.9 | async-start | bytes 5898240 | tf_op jit(solution)/shard_map/reduce_scatter | solution.py:53
  396.9 141.4 %reduce-scatter.7.cloned.1.call-start = ((), (), s32[]{:S(2)}) async-start(), calls=%async_computation.6 | async-start | bytes 5898240 | tf_op jit(solution)/shard_map/reduce_scatter | solution.py:53
  422.8 1.9 copy-start.14
  422.8 159.9 %reduce-scatter.9.cloned.1.call-start = ((), (), s32[]{:S(2)}) async-start(), calls=%async_computation.7 | async-start | bytes 5898240 | tf_op jit(solution)/shard_map/reduce_scatter | solution.py:53
  439.2 155.9 %copy-start.4 = (bf16[2,768,768]{2,1,0:T(8,128)(2,1)S(1)}, bf16[2,768,768]{2,1,0:T(8,128)(2,1)}, u32[]{:S(2)}) copy-start(bf16[2,768,768]{2,1,0:T(8,128)(2,1)} %param.15) | copy-start | bytes 7077892
  439.3 155.8 %copy-start.7 = (bf16[768,768]{1,0:T(8,128)(2,1)S(1)}, bf16[768,768]{1,0:T(8,128)(2,1)}, u32[]{:S(2)}) copy-start(bf16[768,768]{1,0:T(8,128)(2,1)} %reduce-scatter.15.cloned.1.call-done) | copy-start | bytes 3538948
  595.1 9.9 %copy-start.5 = (bf16[2,192,3072]{2,1,0:T(8,128)(2,1)S(1)}, bf16[2,192,3072]{2,1,0:T(8,128)(2,1)}, u32[]{:S(2)}) copy-start(bf16[2,192,3072]{2,1,0:T(8,128)(2,1)} %param.13) | copy-start | bytes 7077892
  595.1 9.9 %copy-start.6 = (bf16[2,192,3072]{2,1,0:T(8,128)(2,1)S(1)}, bf16[2,192,3072]{2,1,0:T(8,128)(2,1)}, u32[]{:S(2)}) copy-start(bf16[2,192,3072]{2,1,0:T(8,128)(2,1)} %param.14) | copy-start | bytes 7077892
  595.1 9.9 %copy-start.8 = (bf16[192,3072]{1,0:T(8,128)(2,1)S(1)}, bf16[192,3072]{1,0:T(8,128)(2,1)}, u32[]{:S(2)}) copy-start(bf16[192,3072]{1,0:T(8,128)(2,1)} %reduce-scatter.11.cloned.1.call-done) | copy-start | bytes 3538948
  595.1 9.9 %copy-start.9 = (bf16[192,3072]{1,0:T(8,128)(2,1)S(1)}, bf16[192,3072]{1,0:T(8,128)(2,1)}, u32[]{:S(2)}) copy-start(bf16[192,3072]{1,0:T(8,128)(2,1)} %reduce-scatter.13.cloned.1.call-done) | copy-start | bytes 3538948
  595.1 9.9 %copy-start.10 = (bf16[192,3072]{1,0:T(8,128)(2,1)S(1)}, bf16[192,3072]{1,0:T(8,128)(2,1)}, u32[]{:S(2)}) copy-start(bf16[192,3072]{1,0:T(8,128)(2,1)} %reduce-scatter.7.cloned.1.call-done) | copy-start | bytes 3538948
  595.2 10.8 %copy-start.11 = (bf16[192,3072]{1,0:T(8,128)(2,1)S(1)}, bf16[192,3072]{1,0:T(8,128)(2,1)}, u32[]{:S(2)}) copy-start(bf16[192,3072]{1,0:T(8,128)(2,1)} %reduce-scatter.9.cloned.1.call-done) | copy-start | bytes 3538948
Sparse Core Ops, SparseCore 0:
  10.5 37.3 all-gather.12
  50.0 34.5 all-gather.14
  86.7 34.5 all-gather.16
  123.2 34.5 all-gather.20
  159.8 34.5 all-gather.22
  196.3 34.5 all-gather.18
  318.1 41.5 reduce-scatter.14
  362.8 41.5 reduce-scatter.16
  407.4 41.5 reduce-scatter.10
  451.9 41.5 reduce-scatter.12
  496.6 41.5 reduce-scatter.6
  541.1 41.5 reduce-scatter.8
where the time goes:
time: 637 us; the launch traced here: 630 us
  matrix products  289 us (45%)
  waiting for transfers between devices  253 us (40%)
  other arithmetic  40.4 us (6%)
  local copies, waits for them, and re-layouts  23.8 us (4%)
  between operations  17.5 us (3%)
    reduce_scatter x6, waiting for transfers between devices, step(): lax.psum_scatter(by_w[name], 'dp', scatter_dimension=0, tiled=True)  136 us
    all_gather x6, waiting for transfers between devices, fetched(): lax.all_gather(w[number], 'dp', axis=0, tiled=True)  115 us
    dot_general x5, matrix products, layer(): gate = jnp.dot(a, w['w_gate'], preferred_element_type=jnp.float32)  105 us
    dot_general x5, matrix products, layer(): up = jnp.dot(a, w['w_up'], preferred_element_type=jnp.float32)  99.3 us
    dot_general x5, matrix products, matmul(): jnp.dot(a, w, preferred_element_type=jnp.float32).astype(jnp.bfloat16)  84.7 us
    convert_element_type x2, other arithmetic, adamw(): return ((w - 0.02 * step).astype(jnp.bfloat16), m, v)  27 us
    unnamed x46, local copies, waits for them, and re-layouts  15.7 us
  transfers between devices with their start and end apart: 12, of which 10 were waited for; matrix products, arithmetic and copies ran while one was open for 36% of the time, Pallas kernels for 0%

commit v1 on v0

v1 whole, which is shorter than its diff:
```python
import functools

import jax
import jax.numpy as jnp
from jax import lax
from jax.experimental import pallas as pl
from jax.experimental.pallas import tpu as pltpu
from jax.sharding import PartitionSpec as P

T, D, FF, L = 2048, 768, 3072, 2
C = 768
TM = 512
RB = D // 4
RH = RB // 2
DH = C // 2
COUNT = 3 * L * D * FF
bf16, f32 = jnp.bfloat16, jnp.float32
NT = (((1,), (1,)), ((), ()))
TN = (((0,), (0,)), ((), ()))
MESH = pl.DeviceIdType.MESH


def dot(a, b, dims=(((1,), (0,)), ((), ()))):
    return lax.dot_general(a, b, dims, preferred_element_type=f32)


def scale_of(wide):
    return lax.rsqrt(jnp.mean(wide * wide, -1, keepdims=True) + 1e-6)


def step_kernel(
    x_hbm, dy_hbm, wg, wu, wd,
    gg_hbm, gu_hbm, gd_hbm, fac, all_g, all_u, all_d, p0_hbm, rd2_hbm, rx_hbm, own_d, rd_d, rx_d,
    h, a0, a1, do, acc, acc_gu, acc_d, w_gu, w_d, act_s, dgu_s, sg, sd, rd3, rd3d, sx, sxd, ssq, ss, ss_src,
    ag_s, ag_r, pe_s, pe_r, ld, wsem, d_s, d_r3, d_r3d, d_r2, d_rd, keep, x_s, x_r, xd_s, xd_r, fsem, fout, ss_s, ss_r,
):
    y, i = lax.axis_index("rep"), lax.axis_index("dp")
    xx, c = i // 2, i % 2
    ix, ip, iq = (1 - xx) * 2 + c, xx * 2 + 1 - c, (1 - xx) * 2 + 1 - c
    at_x, at_p, at_q, at_y = (y, ix), (y, ip), (y, iq), (1 - y, i)

    def remote(src, dst, send, recv, to):
        return pltpu.make_async_remote_copy(
            src_ref=src, dst_ref=dst, send_sem=send, recv_sem=recv, device_id=to, device_id_type=MESH
        )

    def chunk(k):
        return (2 * xx + k) % 4

    def chunk_there(k):
        return (2 * (1 - xx) + k) % 4

    def cols(j):
        return pl.ds(pl.multiple_of(j * C, C), C)

    def rows(start, size):
        return pl.ds(pl.multiple_of(start, 32), size)

    barrier = pltpu.get_barrier_semaphore()
    for other in (at_x, at_p, at_q, at_y):
        pl.semaphore_signal(barrier, inc=1, device_id=other, device_id_type=MESH)
    load_x = pltpu.make_async_copy(x_hbm, h, ld.at[0])
    load_dy = pltpu.make_async_copy(dy_hbm, do, ld.at[1])
    load_x.start()
    load_dy.start()
    pl.semaphore_wait(barrier, 4)

    def region(l, p, src, half, j):
        if p == 8:
            return all_d.at[l, rows(C * src + DH * half, DH), :]
        return (all_g, all_u)[p % 2].at[l, rows(RB * src + RH * half, RH), cols(j)]

    def mine(l, p, src, half):
        return region(l, p, src, half, chunk(p // 2))

    def send_x(l, p):
        if p == 8:
            src = wd.at[l, rows(DH * y, DH), :]
        else:
            src = (wg, wu)[p % 2].at[l, rows(RH * y, RH), cols(chunk_there(p // 2))]
        return remote(src, region(l, p, i, y, chunk_there(p // 2)), ag_s.at[l, p, 0], ag_r.at[l, p, 0], at_x)

    def forward_x(l, *ps):
        for p in ps:
            r = mine(l, p, ix, y)
            remote(r, r, ag_s.at[l, p, 0], ag_r.at[l, p, 0], at_x).wait_recv()
            remote(r, r, ag_s.at[l, p, 1], ag_r.at[l, p, 1], at_y).start()
            remote(r, r, ag_s.at[l, p, 2], ag_r.at[l, p, 2], at_p).start()

    def forward_y(l, *ps):
        for p in ps:
            r = mine(l, p, ix, 1 - y)
            remote(r, r, ag_s.at[l, p, 1], ag_r.at[l, p, 1], at_y).wait_recv()
            remote(r, r, ag_s.at[l, p, 3], ag_r.at[l, p, 3], at_p).start()

    def landed(l, *ps):
        for p in ps:
            for which, half in ((2, y), (3, 1 - y)):
                r = mine(l, p, iq, half)
                remote(r, r, ag_s.at[l, p, which], ag_r.at[l, p, which], at_p).wait_recv()

    def to_peer(l, m):
        src = (wg, wu, wd)[m].at[l]
        dst = (all_g.at[l, rows(RB * i, RB), :], all_u.at[l, rows(RB * i, RB), :], all_d.at[l, rows(C * i, C), :])[m]
        return remote(src, dst, pe_s.at[l, m], pe_r.at[l, m], at_p)

    def from_peer(l):
        for m in range(3):
            to_peer(l, m).wait_recv()

    for l in range(L):
        for p in (0, 1, 2, 3, 8, 4, 5, 6, 7):
            send_x(l, p).start()
        for m in range(3):
            to_peer(l, m).start()

    def stage(l, k, start):
        j, slot = chunk(k), k % 2
        for m, (own, gathered) in enumerate(((wg, all_g), (wu, all_u))):
            for n, (src, row, size) in enumerate(
                (
                    (own.at[l, :, cols(j)], RB * i, RB),
                    (gathered.at[l, rows(RB * ip, RB), cols(j)], RB * ip, RB),
                    (gathered.at[l, rows(2 * RB * (1 - xx), 2 * RB), cols(j)], 2 * RB * (1 - xx), 2 * RB),
                )
            ):
                copy = pltpu.make_async_copy(
                    src, w_gu.at[slot, rows(row, size), m * C : (m + 1) * C], wsem.at[slot, 3 * m + n]
                )
                copy.start() if start else copy.wait()
        theirs = pltpu.make_async_copy(all_d.at[l, rows(C * j, C), :], w_d.at[slot], wsem.at[slot, 6])
        if start:

            @pl.when(j == i)
            def _():
                pltpu.make_async_copy(wd.at[l], w_d.at[slot], wsem.at[slot, 6]).start()

            @pl.when(j != i)
            def _():
                theirs.start()
        else:
            theirs.wait()

    def tile(t):
        return pl.ds(pl.multiple_of(t * TM, TM), TM)

    def clear(ref, size):
        n = ref.shape[0] // size

        @pl.loop(0, n)
        def _(t):
            ref[pl.ds(pl.multiple_of(t * size, size), size), :] = jnp.zeros((size, ref.shape[1]), ref.dtype)

    clear(acc, 256)
    clear(acc_gu, 128)
    clear(acc_d, 128)
    ssq[...] = jnp.zeros_like(ssq)
    load_x.wait()

    @pl.loop(0, T // 256)
    def _(t):
        r = pl.ds(pl.multiple_of(t * 256, 256), 256)
        wide = h[r, :].astype(f32)
        a0[r, :] = (wide * scale_of(wide)).astype(bf16)

    @pl.loop(0, 4)
    def _(k):
        @pl.when(k == 0)
        def _():
            forward_x(0, 0, 1, 2, 3)
            forward_y(0, 0, 1)
            from_peer(0)
            landed(0, 0, 1)

        @pl.when(k == 1)
        def _():
            forward_y(0, 2, 3)
            forward_x(0, 8)
            landed(0, 2, 3)

        @pl.when(k == 2)
        def _():
            forward_x(0, 4, 5, 6, 7)
            forward_y(0, 8)
            landed(0, 8)
            forward_y(0, 4, 5)
            forward_x(1, 0, 1)
            landed(0, 4, 5)

        @pl.when(k == 3)
        def _():
            forward_y(0, 6, 7)
            forward_x(1, 2, 3)
            landed(0, 6, 7)

        stage(0, k, True)
        stage(0, k, False)

        @pl.loop(0, T // TM)
        def _(t):
            r = tile(t)
            gu = dot(a0[r, :], w_gu[k % 2])
            gate, up = gu[:, :C], gu[:, C:]
            act = (gate * jax.nn.sigmoid(gate) * up).astype(bf16)
            acc[r, :] += dot(act, w_d[k % 2])

    forward_y(1, 0, 1)
    from_peer(1)
    landed(1, 0, 1)
    stage(1, 0, True)
    load_dy.wait()

    @pl.loop(0, T // 256)
    def _(t):
        r = pl.ds(pl.multiple_of(t * 256, 256), 256)
        wide = (h[r, :].astype(f32) + acc[r, :].astype(bf16).astype(f32)).astype(bf16)
        h[r, :] = wide
        wide = wide.astype(f32)
        a1[r, :] = (wide * scale_of(wide)).astype(bf16)
        acc[r, :] = jnp.zeros((256, D), f32)

    def d_copies(l, k, act):
        j, s2 = chunk(k), k % 2
        act(remote(sg.at[3], rd3.at[s2], d_s.at[0], d_r3.at[s2], at_p))

        @pl.when(k >= 2)
        def _():
            act(remote(sd.at[rows(DH * (1 - c), DH), :], rd3d.at[s2], d_s.at[1], d_r3d.at[s2], at_p))

        act(remote(sg.at[2], rd2_hbm.at[l, j], d_s.at[2], d_r2.at[l, j], at_p))

        @pl.when((k < 2) & (c != k))
        def _():
            act(remote(sd, rd_d.at[l], d_s.at[3], d_rd.at[l], at_p))

        act(pltpu.make_async_copy(sg.at[0], p0_hbm.at[l, j], keep.at[0]))

        @pl.when((k < 2) & (c == k))
        def _():
            act(pltpu.make_async_copy(sd, own_d.at[l], keep.at[1]))

    def start(copy):
        copy.start()

    def drain(copy):
        copy.wait_send() if copy.is_remote else copy.wait()

    def send_sums(l, k):
        for r, dest in ((3, iq), (1, ix), (2, ip), (0, i)):
            for m in range(2):
                sg[r, RB * m : RB * (m + 1), :] = acc_gu[rows(RB * dest, RB), m * C : (m + 1) * C].astype(bf16)
        sd[...] = acc_d[...].astype(bf16)
        clear(acc_gu, 128)
        clear(acc_d, 128)
        d_copies(l, k, start)

    def x_copy(l, k):
        s4 = k
        return remote(sx.at[s4], rx_hbm.at[l, chunk(k)], x_s.at[s4], x_r.at[l, chunk(k)], at_x)

    def xd_copy(l, k):
        to = (y, 2 * (1 - xx) + k - 2)
        return remote(sxd.at[l, k - 2], rx_d.at[l, rows(DH * c, DH), :], xd_s.at[l, k - 2], xd_r.at[l, c], to)

    def across(l, k, again):
        s2 = k % 2
        remote(sg.at[3], rd3.at[s2], d_s.at[0], d_r3.at[s2], at_p).wait_recv()
        if again:
            x_copy(l, k).wait_send()
        sx[k] = (sg[1].astype(f32) + rd3[s2].astype(f32)).astype(bf16)

        @pl.when(k >= 2)
        def _():
            remote(sd.at[rows(DH * (1 - c), DH), :], rd3d.at[s2], d_s.at[1], d_r3d.at[s2], at_p).wait_recv()
            sxd[l, k - 2] = (sd[rows(DH * c, DH), :].astype(f32) + rd3d[s2].astype(f32)).astype(bf16)

        x_copy(l, k).start()

        @pl.when(k >= 2)
        def _():
            xd_copy(l, k).start()

        d_copies(l, k, drain)

    def add_up(parts, puts):
        for n, part in enumerate(parts):
            pltpu.make_async_copy(part, h.at[n * 384 : (n + 1) * 384, :], fsem.at[n]).start()
        for n, part in enumerate(parts):
            pltpu.make_async_copy(part, h.at[n * 384 : (n + 1) * 384, :], fsem.at[n]).wait()
        for r in range(0, 384, 128):
            g = h[r : r + 128, :].astype(f32) + h[384 + r : 512 + r, :].astype(f32) + h[768 + r : 896 + r, :].astype(f32)
            g = g.astype(bf16)
            h[1152 + r : 1280 + r, :] = g
            g = g.astype(f32)
            ssq[...] += jnp.sum((g * g).reshape(16, 8, D), axis=0)
        outs = []
        for n, (row, size, dst) in enumerate(puts):
            outs.append(pltpu.make_async_copy(h.at[1152 + row : 1152 + row + size, :], dst, fout.at[n]))
        for out in outs:
            out.start()
        for out in outs:
            out.wait()

    def finish_gu(l, k):
        j = chunk_there(k)
        remote(sg.at[2], rd2_hbm.at[l, j], d_s.at[2], d_r2.at[l, j], at_p).wait_recv()
        remote(sx.at[0], rx_hbm.at[l, j], x_s.at[0], x_r.at[l, j], at_x).wait_recv()
        add_up(
            [p0_hbm.at[l, j], rd2_hbm.at[l, j], rx_hbm.at[l, j]],
            [(0, RB, gg_hbm.at[l, :, cols(j)]), (RB, RB, gu_hbm.at[l, :, cols(j)])],
        )

    def finish_d(l):
        remote(sd, rd_d.at[l], d_s.at[3], d_rd.at[l], at_p).wait_recv()
        for half in range(2):
            part = rx_d.at[l, half * DH : (half + 1) * DH, :]
            remote(sxd.at[0, 0], part, xd_s.at[0, 0], xd_r.at[l, half], at_x).wait_recv()
        for half in range(2):
            r = slice(half * DH, (half + 1) * DH)
            add_up([own_d.at[l, r, :], rd_d.at[l, r, :], rx_d.at[l, r, :]], [(0, DH, gd_hbm.at[l, r, :])])

    def backward(l, a, k, t):
        r, slot = tile(t), k % 2
        gu = dot(a[r, :], w_gu[slot])
        dact = dot(do[r, :], w_d[slot], NT).astype(bf16).astype(f32)
        gate, up = gu[:, :C], gu[:, C:]
        sig = jax.nn.sigmoid(gate)
        silu = gate * sig
        act_s[...] = (silu * up).astype(bf16)
        dgu_s[:, C:] = (dact * silu).astype(bf16)
        dgu_s[:, :C] = (dact * up * (sig + silu * (1.0 - sig))).astype(bf16)
        if l:
            acc[r, :] += dot(dgu_s[...], w_gu[slot], NT)
        acc_gu[...] += dot(a[r, :], dgu_s[...], TN)
        acc_d[...] += dot(act_s[...], do[r, :], TN)

    stage(1, 0, False)

    @pl.loop(0, 4)
    def _(k):
        @pl.when(k > 0)
        def _():
            stage(1, k, False)

        @pl.loop(0, T // TM)
        def _(t):
            backward(1, a1, k, t)

            @pl.when((t == 0) & (k > 0))
            def _():
                across(1, k - 1, False)

            @pl.when((t == 1) & (k == 0))
            def _():
                forward_y(1, 2, 3)
                forward_x(1, 8, 4, 5)

            @pl.when((t == 2) & (k == 0))
            def _():
                forward_x(1, 6, 7)
                landed(1, 2, 3)
                stage(1, 1, True)

            @pl.when((t == 1) & (k == 1))
            def _():
                forward_y(1, 8, 4, 5, 6, 7)

            @pl.when((t == 2) & (k == 1))
            def _():
                landed(1, 8, 4, 5)
                stage(1, 2, True)

            @pl.when((t == 2) & (k == 2))
            def _():
                landed(1, 6, 7)
                stage(1, 3, True)

            @pl.when((t == 2) & (k == 3))
            def _():
                stage(0, 0, True)

        send_sums(1, k)

    @pl.loop(0, T // 256)
    def _(t):
        r = pl.ds(pl.multiple_of(t * 256, 256), 256)
        wide = h[r, :].astype(f32)
        scale = scale_of(wide)
        da = acc[r, :].astype(bf16).astype(f32)
        mix = jnp.sum(da * wide, -1, keepdims=True) * (scale * scale * scale / D)
        back = (da * scale - wide * mix).astype(bf16)
        do[r, :] = (do[r, :].astype(f32) + back.astype(f32)).astype(bf16)

    @pl.loop(0, 4)
    def _(k):
        stage(0, k, False)

        @pl.loop(0, T // TM)
        def _(t):
            backward(0, a0, k, t)

            @pl.when((t == 0) & (k == 0))
            def _():
                across(1, 3, False)

            @pl.when((t == 0) & (k > 0))
            def _():
                across(0, k - 1, True)

            @pl.when((t == 2) & (k < 3))
            def _():
                stage(0, k + 1, True)

            @pl.when(t == 2)
            def _():
                finish_gu(1, k)

        send_sums(0, k)

    across(0, 3, True)
    finish_d(1)

    @pl.loop(0, 4)
    def _(k):
        finish_gu(0, k)

    finish_d(0)

    part = ssq[:, :128]
    for n in range(1, D // 128):
        part = part + ssq[:, n * 128 : (n + 1) * 128]
    ss_src[...] = part
    for l in range(L):
        for p in range(9):
            for which, (src, half, to) in enumerate(((ix, y, at_x), (ix, y, at_y), (ix, y, at_p), (ix, 1 - y, at_p))):
                if which == 0:
                    send_x(l, p).wait_send()
                else:
                    r = mine(l, p, src, half)
                    remote(r, r, ag_s.at[l, p, which], ag_r.at[l, p, which], to).wait_send()
        for m in range(3):
            to_peer(l, m).wait_send()
        for k in (2, 3):
            xd_copy(l, k).wait_send()
    for k in range(4):
        x_copy(0, k).wait_send()
    tells = [
        remote(ss_src, ss.at[i], ss_s.at[n], ss_r.at[i], to) for n, to in enumerate((at_x, at_p, at_q))
    ]
    for tell in tells:
        tell.start()
    for src in (ix, ip, iq):
        remote(ss_src, ss.at[src], ss_s.at[0], ss_r.at[src], at_x).wait_recv()
    for tell in tells:
        tell.wait_send()
    ss[i] = part
    total = jnp.sum(ss[0] + ss[1] + ss[2] + ss[3])
    fac[...] = jnp.minimum(1.0, 0.5 * lax.rsqrt(jnp.full((8, 128), total / COUNT + 1e-30, f32)))


def gradients(x, dy, wg, wu, wd):
    hbm = pl.BlockSpec(memory_space=pl.ANY)
    vmem = pl.BlockSpec(memory_space=pltpu.VMEM)
    out = lambda *shape: jax.ShapeDtypeStruct(shape, bf16)
    dma = lambda *shape: pltpu.SemaphoreType.DMA(shape)
    return pl.pallas_call(
        step_kernel,
        in_specs=[hbm] * 5,
        out_specs=[hbm] * 3 + [vmem] + [hbm] * 9,
        out_shape=[
            out(L, RB, FF), out(L, RB, FF), out(L, C, D), jax.ShapeDtypeStruct((8, 128), f32),
            out(L, D, FF), out(L, D, FF), out(L, FF, D),
            out(L, 4, 2 * RB, C), out(L, 4, 2 * RB, C), out(L, 4, 2 * RB, C),
            out(L, C, D), out(L, C, D), out(L, C, D),
        ],
        scratch_shapes=[
            pltpu.VMEM((T, D), bf16), pltpu.VMEM((T, D), bf16), pltpu.VMEM((T, D), bf16), pltpu.VMEM((T, D), bf16),
            pltpu.VMEM((T, D), f32), pltpu.VMEM((D, 2 * C), f32), pltpu.VMEM((C, D), f32),
            pltpu.VMEM((2, D, 2 * C), bf16), pltpu.VMEM((2, C, D), bf16),
            pltpu.VMEM((TM, C), bf16), pltpu.VMEM((TM, 2 * C), bf16),
            pltpu.VMEM((4, 2 * RB, C), bf16), pltpu.VMEM((C, D), bf16),
            pltpu.VMEM((2, 2 * RB, C), bf16), pltpu.VMEM((2, DH, D), bf16),
            pltpu.VMEM((4, 2 * RB, C), bf16), pltpu.VMEM((2, 2, DH, D), bf16),
            pltpu.VMEM((8, D), f32), pltpu.VMEM((4, 8, 128), f32), pltpu.VMEM((8, 128), f32),
            dma(L, 9, 4), dma(L, 9, 4), dma(L, 3), dma(L, 3), dma(2), dma(2, 7),
            dma(4), dma(2), dma(2), dma(L, 4), dma(L), dma(2), dma(4), dma(L, 4), dma(L, 2), dma(L, 2),
            dma(3), dma(2), dma(3), dma(4),
        ],
        compiler_params=pltpu.CompilerParams(
            collective_id=0, has_side_effects=True, vmem_limit_bytes=63 * 2**20
        ),
        name="train_step",
    )(x, dy, wg, wu, wd)


def adamw_kernel(*refs):
    fac, ins, outs = refs[0], refs[1:13], refs[13:]
    factor = fac[0:1, 0:1]
    for n in range(3):
        g, w, m, v = (ins[3 * which + n] for which in range(4))
        grad = g[0].astype(f32) * factor
        new_m = 0.9 * m[0] + 0.1 * grad
        new_v = 0.95 * v[0] + 0.05 * grad * grad
        wide = w[0].astype(f32)
        outs[n][0] = (wide - 0.02 * (new_m * lax.rsqrt(new_v + 1e-8) + 0.1 * wide)).astype(bf16)
        outs[3 + n][0] = new_m
        outs[6 + n][0] = new_v


def adamw(factor, g, w, m, v):
    wide = pl.BlockSpec((1, RB // 12, FF), lambda t: (t // 12, t % 12, 0))
    tall = pl.BlockSpec((1, C // 12, D), lambda t: (t // 12, t % 12, 0))
    specs = [wide, wide, tall]
    shapes = lambda dtype: [jax.ShapeDtypeStruct(a.shape, dtype) for a in w]
    return pl.pallas_call(
        adamw_kernel,
        grid=(24,),
        in_specs=[pl.BlockSpec((8, 128), lambda t: (0, 0))] + specs * 4,
        out_specs=specs * 3,
        out_shape=shapes(bf16) + shapes(f32) + shapes(f32),
        compiler_params=pltpu.CompilerParams(vmem_limit_bytes=63 * 2**20),
        name="adamw",
    )(factor, *g, *w, *m, *v)


def solution(mesh):
    def step(x, dy, *arrays):
        w, m, v = (arrays[n : n + 3] for n in (0, 3, 6))
        gg, gu, gd, factor, *_ = gradients(x[0], dy[0], *w)
        return tuple(adamw(factor, (gg, gu, gd), w, m, v))

    states, cut = P(("rep", "dp"), None, None), P(None, "dp", None)
    return jax.shard_map(
        step,
        mesh=mesh,
        in_specs=(states, states) + (cut,) * 9,
        out_specs=(P("rep", "dp", None),) * 9,
        check_vma=False,
    )
```

time: 637 us -> 348 us (0.55)
  Pallas kernels: 0 us -> 347 us
  matrix products: 289 us -> 0 us
  waiting for transfers between devices: 253 us -> 0 us
  other arithmetic: 40.4 us -> 0 us
  local copies, waits for them, and re-layouts: 23.8 us -> 0 us
  between operations: 17.5 us -> 0.81 us
    pallas_call x0 -> x2, Pallas kernels: none -> 347 us  [the longest x1 313 us: gradients(): pl.pallas_call(step_kernel, in_specs=[hbm] * 5, out_specs=[hbm] * 3 + [vm...]
    dot_general x15 -> x0, matrix products: 289 us -> none  [the longest x5 105 us: layer(): gate = jnp.dot(a, w['w_gate'], preferred_element_type=jnp.float32)]
    reduce_scatter x6 -> x0, waiting for transfers between devices: 136 us -> none  [step(): lax.psum_scatter(by_w[name], 'dp', scatter_dimension=0, tiled=True)]
    all_gather x6 -> x0, waiting for transfers between devices: 115 us -> none  [fetched(): lax.all_gather(w[number], 'dp', axis=0, tiled=True)]
    convert_element_type x2 -> x0, other arithmetic: 27 us -> none  [adamw(): return ((w - 0.02 * step).astype(jnp.bfloat16), m, v)]
    unnamed x46 -> x0, local copies, waits for them, and re-layouts: 15.7 us -> none
    reduce_sum x4 -> x0, other arithmetic: 11.1 us -> none  [the longest x3 10.5 us: step(): squares = lax.psum(sum((jnp.sum(g * g) for g in gradients)), 'dp')]
    slice x3 -> x0, local copies, waits for them, and re-layouts: 8.07 us -> none  [fetched(): w[number]]
  transfers between devices with their start and end apart: 12 -> 0, of which waited for: 10 -> 0; matrix products, arithmetic and copies ran while one was open for 36% -> 0% of each run, Pallas kernels for 0% -> 0%
where the time goes in v1:
time: 348 us
  Pallas kernels  347 us (100%)
    pallas_call x1, Pallas kernels, gradients(): pl.pallas_call(step_kernel, in_specs=[hbm] * 5, out_specs=[hbm] * 3 + [vm...  313 us
    pallas_call x1, Pallas kernels, adamw(): pl.pallas_call(adamw_kernel, grid=(24,), in_specs=[pl.BlockSpec((8, 128),...  33.8 us

profile of v1, /device:TPU:0, one launch (start us, length us, event | category | flops | bytes accessed | tf_op | source)
XLA Modules:
  0.0 347.5 jit_solution(10329967480908158115)
XLA Ops:
  0.6 312.9 %train_step.1 = (bf16[2,192,3072]{2,1,0:T(8,128)(2,1)}, bf16[2,192,3072]{2,1,0:T(8,128)(2,1)}, bf16[2,768,768]{2,1,0:T(8,128)(2,1)}, f32[8,128]{1,0:T(8,128)}, b...) custom-call(bf16[2048,768]{1,0:T(8,128)(2,1)} %bitcast.2, ...), custom_call_target="tpu_custom_call" | custom-call | tf_op jit(solution)/shard_map/train_step/pallas_call | solution.py:466
  313.5 33.8 %adamw.1 = (bf16[2,192,3072]{2,1,0:T(8,128)(2,1)}, bf16[2,192,3072]{2,1,0:T(8,128)(2,1)}, bf16[2,768,768]{2,1,0:T(8,128)(2,1)}, f32[2,192,3072]{2,1,0:T(8,128)},...) custom-call(f32[8,128]{1,0:T(8,128)} %get-tuple-element.13.refs_0_, ...), custom_call_target="tpu_custom_call" | custom-call | tf_op jit(solution)/shard_map/adamw/pallas_call | solution.py:515

commit v2 on v1

--- a/solution.py
+++ b/solution.py
@@ -13,6 +13,8 @@
 RB = D // 4
 RH = RB // 2
 DH = C // 2
+DQ = C // 4
+N = 4
 COUNT = 3 * L * D * FF
 bf16, f32 = jnp.bfloat16, jnp.float32
 NT = (((1,), (1,)), ((), ()))
@@ -44,11 +46,20 @@
             src_ref=src, dst_ref=dst, send_sem=send, recv_sem=recv, device_id=to, device_id_type=MESH
         )
 
-    def chunk(k):
+    def near_first(k):
         return (2 * xx + k) % 4
 
-    def chunk_there(k):
+    def far_first(k):
         return (2 * (1 - xx) + k) % 4
+
+    def start(copy):
+        copy.start()
+
+    def drain(copy):
+        copy.wait_send() if copy.is_remote else copy.wait()
+
+    def at(t, n, k, m, work):
+        pl.when((t == n) & (k == m))(work)
 
     def cols(j):
         return pl.ds(pl.multiple_of(j * C, C), C)
@@ -66,19 +77,33 @@
     pl.semaphore_wait(barrier, 4)
 
     def region(l, p, src, half, j):
-        if p == 8:
-            return all_d.at[l, rows(C * src + DH * half, DH), :]
+        if p >= 8:
+            return all_d.at[l, rows(C * (src // 2 * 2 + p - 8) + DH * half + DQ * (src % 2), DQ), :]
         return (all_g, all_u)[p % 2].at[l, rows(RB * src + RH * half, RH), cols(j)]
 
     def mine(l, p, src, half):
-        return region(l, p, src, half, chunk(p // 2))
-
-    def send_x(l, p):
-        if p == 8:
-            src = wd.at[l, rows(DH * y, DH), :]
+        return region(l, p, src, half, (near_first, far_first)[l](p // 2))
+
+    def send_x(l, p, act):
+        j = (far_first, near_first)[l](p // 2)
+        there = region(l, p, i, y, j)
+
+        def copy(src):
+            return remote(src, there, ag_s.at[l, p, 0], ag_r.at[l, p, 0], at_x)
+
+        if p < 8:
+            act(copy((wg, wu)[p % 2].at[l, rows(RH * y, RH), cols(j)]))
+        elif act is start:
+
+            @pl.when(c == p - 8)
+            def _():
+                act(copy(wd.at[l, rows(DH * y + DQ * c, DQ), :]))
+
+            @pl.when(c != p - 8)
+            def _():
+                act(copy(there))
         else:
-            src = (wg, wu)[p % 2].at[l, rows(RH * y, RH), cols(chunk_there(p // 2))]
-        return remote(src, region(l, p, i, y, chunk_there(p // 2)), ag_s.at[l, p, 0], ag_r.at[l, p, 0], at_x)
+            act(copy(there))
 
     def forward_x(l, *ps):
         for p in ps:
@@ -108,14 +133,14 @@
         for m in range(3):
             to_peer(l, m).wait_recv()
 
+    for p in range(6):
+        send_x(0, p, start)
     for l in range(L):
-        for p in (0, 1, 2, 3, 8, 4, 5, 6, 7):
-            send_x(l, p).start()
         for m in range(3):
             to_peer(l, m).start()
 
-    def stage(l, k, start):
-        j, slot = chunk(k), k % 2
+    def stage_gu(l, k, j, act):
+        slot = k % 2
         for m, (own, gathered) in enumerate(((wg, all_g), (wu, all_u))):
             for n, (src, row, size) in enumerate(
                 (
@@ -127,9 +152,12 @@
                 copy = pltpu.make_async_copy(
                     src, w_gu.at[slot, rows(row, size), m * C : (m + 1) * C], wsem.at[slot, 3 * m + n]
                 )
-                copy.start() if start else copy.wait()
+                act(copy)
+
+    def stage_d(l, k, j, act):
+        slot = k % 2
         theirs = pltpu.make_async_copy(all_d.at[l, rows(C * j, C), :], w_d.at[slot], wsem.at[slot, 6])
-        if start:
+        if act is start:
 
             @pl.when(j == i)
             def _():
@@ -139,7 +167,11 @@
             def _():
                 theirs.start()
         else:
-            theirs.wait()
+            act(theirs)
+
+    def stage(l, k, j, act):
+        stage_gu(l, k, j, act)
+        stage_d(l, k, j, act)
 
     def tile(t):
         return pl.ds(pl.multiple_of(t * TM, TM), TM)
@@ -163,51 +195,97 @@
         wide = h[r, :].astype(f32)
         a0[r, :] = (wide * scale_of(wide)).astype(bf16)
 
+    def forward(k, t):
+        r = tile(t)
+        gu = dot(a0[r, :], w_gu[k % 2])
+        gate, up = gu[:, :C], gu[:, C:]
+        act = (gate * jax.nn.sigmoid(gate) * up).astype(bf16)
+        acc[r, :] += dot(act, w_d[k % 2])
+
+    forward_x(0, 0, 1)
+    from_peer(0)
+    for p in (8, 6, 7, 9):
+        send_x(0, p, start)
+    forward_x(0, 2, 3)
+    forward_y(0, 0, 1)
+    landed(0, 0, 1)
+    stage(0, 0, near_first(0), start)
+
     @pl.loop(0, 4)
     def _(k):
-        @pl.when(k == 0)
-        def _():
-            forward_x(0, 0, 1, 2, 3)
-            forward_y(0, 0, 1)
-            from_peer(0)
-            landed(0, 0, 1)
-
-        @pl.when(k == 1)
-        def _():
-            forward_y(0, 2, 3)
-            forward_x(0, 8)
-            landed(0, 2, 3)
-
-        @pl.when(k == 2)
-        def _():
-            forward_x(0, 4, 5, 6, 7)
-            forward_y(0, 8)
-            landed(0, 8)
-            forward_y(0, 4, 5)
-            forward_x(1, 0, 1)
-            landed(0, 4, 5)
-
-        @pl.when(k == 3)
-        def _():
-            forward_y(0, 6, 7)
-            forward_x(1, 2, 3)
-            landed(0, 6, 7)
-
-        stage(0, k, True)
-        stage(0, k, False)
+        stage(0, k, near_first(k), drain)
 
         @pl.loop(0, T // TM)
         def _(t):
-            r = tile(t)
-            gu = dot(a0[r, :], w_gu[k % 2])
-            gate, up = gu[:, :C], gu[:, C:]
-            act = (gate * jax.nn.sigmoid(gate) * up).astype(bf16)
-            acc[r, :] += dot(act, w_d[k % 2])
-
-    forward_y(1, 0, 1)
-    from_peer(1)
-    landed(1, 0, 1)
-    stage(1, 0, True)
+            forward(k, t)
+
+            @functools.partial(at, t, 0, k, 0)
+            def _():
+                forward_y(0, 2, 3)
+                forward_x(0, 4, 5)
+
+            @functools.partial(at, t, 1, k, 0)
+            def _():
+                from_peer(1)
+                for p in (0, 1, 8, 2, 3, 9, 4, 5, 6, 7):
+                    send_x(1, p, start)
+
+            @functools.partial(at, t, 2, k, 0)
+            def _():
+                landed(0, 2, 3)
+                stage(0, 1, near_first(1), start)
+
+            @functools.partial(at, t, 3, k, 0)
+            def _():
+                forward_x(0, 8)
+                forward_y(0, 4, 5)
+
+            @functools.partial(at, t, 1, k, 1)
+            def _():
+                landed(0, 4, 5)
+                stage_gu(0, 2, near_first(2), start)
+
+            @functools.partial(at, t, 2, k, 1)
+            def _():
+                forward_x(0, 6, 7)
+                forward_y(0, 8)
+
+            @functools.partial(at, t, 3, k, 1)
+            def _():
+                landed(0, 8)
+                stage_d(0, 2, near_first(2), start)
+
+            @functools.partial(at, t, 0, k, 2)
+            def _():
+                forward_x(0, 9)
+                forward_y(0, 6, 7)
+
+            @functools.partial(at, t, 2, k, 2)
+            def _():
+                landed(0, 6, 7)
+                stage_gu(0, 3, near_first(3), start)
+
+            @functools.partial(at, t, 3, k, 2)
+            def _():
+                forward_y(0, 9)
+                forward_x(1, 0, 1)
+                landed(0, 9)
+                stage_d(0, 3, near_first(3), start)
+
+            @functools.partial(at, t, 1, k, 3)
+            def _():
+                forward_y(1, 0, 1)
+                forward_x(1, 8)
+
+            @functools.partial(at, t, 3, k, 3)
+            def _():
+                forward_y(1, 8)
+                forward_x(1, 2, 3)
+                landed(1, 0, 1)
+                stage_gu(1, 0, far_first(0), start)
+                landed(1, 8)
+                stage_d(1, 0, far_first(0), start)
+
     load_dy.wait()
 
     @pl.loop(0, T // 256)
@@ -220,30 +298,24 @@
         acc[r, :] = jnp.zeros((256, D), f32)
 
     def d_copies(l, k, act):
-        j, s2 = chunk(k), k % 2
+        j, s2 = far_first(k), k % 2
         act(remote(sg.at[3], rd3.at[s2], d_s.at[0], d_r3.at[s2], at_p))
 
-        @pl.when(k >= 2)
+        @pl.when(k < 2)
         def _():
             act(remote(sd.at[rows(DH * (1 - c), DH), :], rd3d.at[s2], d_s.at[1], d_r3d.at[s2], at_p))
 
         act(remote(sg.at[2], rd2_hbm.at[l, j], d_s.at[2], d_r2.at[l, j], at_p))
 
-        @pl.when((k < 2) & (c != k))
+        @pl.when((k >= 2) & (c != k - 2))
         def _():
             act(remote(sd, rd_d.at[l], d_s.at[3], d_rd.at[l], at_p))
 
         act(pltpu.make_async_copy(sg.at[0], p0_hbm.at[l, j], keep.at[0]))
 
-        @pl.when((k < 2) & (c == k))
+        @pl.when((k >= 2) & (c == k - 2))
         def _():
             act(pltpu.make_async_copy(sd, own_d.at[l], keep.at[1]))
-
-    def start(copy):
-        copy.start()
-
-    def drain(copy):
-        copy.wait_send() if copy.is_remote else copy.wait()
 
     def send_sums(l, k):
         for r, dest in ((3, iq), (1, ix), (2, ip), (0, i)):
@@ -255,12 +327,12 @@
         d_copies(l, k, start)
 
     def x_copy(l, k):
-        s4 = k
-        return remote(sx.at[s4], rx_hbm.at[l, chunk(k)], x_s.at[s4], x_r.at[l, chunk(k)], at_x)
+        j = far_first(k)
+        return remote(sx.at[k], rx_hbm.at[l, j], x_s.at[k], x_r.at[l, j], at_x)
 
     def xd_copy(l, k):
-        to = (y, 2 * (1 - xx) + k - 2)
-        return remote(sxd.at[l, k - 2], rx_d.at[l, rows(DH * c, DH), :], xd_s.at[l, k - 2], xd_r.at[l, c], to)
+        to = (y, 2 * (1 - xx) + k)
+        return remote(sxd.at[l, k], rx_d.at[l, rows(DH * c, DH), :], xd_s.at[l, k], xd_r.at[l, c], to)
 
     def across(l, k, again):
         s2 = k % 2
@@ -269,55 +341,73 @@
             x_copy(l, k).wait_send()
         sx[k] = (sg[1].astype(f32) + rd3[s2].astype(f32)).astype(bf16)
 
-        @pl.when(k >= 2)
+        @pl.when(k < 2)
         def _():
             remote(sd.at[rows(DH * (1 - c), DH), :], rd3d.at[s2], d_s.at[1], d_r3d.at[s2], at_p).wait_recv()
-            sxd[l, k - 2] = (sd[rows(DH * c, DH), :].astype(f32) + rd3d[s2].astype(f32)).astype(bf16)
+            sxd[l, k] = (sd[rows(DH * c, DH), :].astype(f32) + rd3d[s2].astype(f32)).astype(bf16)
 
         x_copy(l, k).start()
 
-        @pl.when(k >= 2)
+        @pl.when(k < 2)
         def _():
             xd_copy(l, k).start()
 
         d_copies(l, k, drain)
 
+    def bring(n, part, act):
+        act(pltpu.make_async_copy(part, h.at[n * 384 : (n + 1) * 384, :], fsem.at[n]))
+
+    def put(n, dst, act):
+        act(pltpu.make_async_copy(h.at[1152 + RB * n : 1152 + RB * (n + 1), :], dst, fout.at[n]))
+
     def add_up(parts, puts):
         for n, part in enumerate(parts):
-            pltpu.make_async_copy(part, h.at[n * 384 : (n + 1) * 384, :], fsem.at[n]).start()
-        for n, part in enumerate(parts):
-            pltpu.make_async_copy(part, h.at[n * 384 : (n + 1) * 384, :], fsem.at[n]).wait()
+            bring(n, part, drain)
         for r in range(0, 384, 128):
             g = h[r : r + 128, :].astype(f32) + h[384 + r : 512 + r, :].astype(f32) + h[768 + r : 896 + r, :].astype(f32)
             g = g.astype(bf16)
             h[1152 + r : 1280 + r, :] = g
             g = g.astype(f32)
             ssq[...] += jnp.sum((g * g).reshape(16, 8, D), axis=0)
-        outs = []
-        for n, (row, size, dst) in enumerate(puts):
-            outs.append(pltpu.make_async_copy(h.at[1152 + row : 1152 + row + size, :], dst, fout.at[n]))
-        for out in outs:
-            out.start()
-        for out in outs:
-            out.wait()
-
-    def finish_gu(l, k):
-        j = chunk_there(k)
-        remote(sg.at[2], rd2_hbm.at[l, j], d_s.at[2], d_r2.at[l, j], at_p).wait_recv()
-        remote(sx.at[0], rx_hbm.at[l, j], x_s.at[0], x_r.at[l, j], at_x).wait_recv()
-        add_up(
-            [p0_hbm.at[l, j], rd2_hbm.at[l, j], rx_hbm.at[l, j]],
-            [(0, RB, gg_hbm.at[l, :, cols(j)]), (RB, RB, gu_hbm.at[l, :, cols(j)])],
-        )
-
-    def finish_d(l):
+        for n, dst in enumerate(puts):
+            put(n, dst, start)
+
+    def put_done():
+        for n in range(2):
+            put(n, gg_hbm.at[0, :, 0:C], drain)
+
+    def gu_parts(l, k):
+        j = near_first(k)
+        return [p0_hbm.at[l, j], rd2_hbm.at[l, j], rx_hbm.at[l, j]]
+
+    def bring_gu(l, k):
+        j = near_first(k)
+        parts = gu_parts(l, k)
+        remote(sg.at[2], parts[1], d_s.at[2], d_r2.at[l, j], at_p).wait_recv()
+        bring(0, parts[0], start)
+        bring(1, parts[1], start)
+        remote(sx.at[0], parts[2], x_s.at[0], x_r.at[l, j], at_x).wait_recv()
+        bring(2, parts[2], start)
+
+    def add_gu(l, k):
+        j = near_first(k)
+        add_up(gu_parts(l, k), [gg_hbm.at[l, :, cols(j)], gu_hbm.at[l, :, cols(j)]])
+
+    def d_parts(l, half):
+        r = rows(half * DH, DH)
+        return [own_d.at[l, r, :], rd_d.at[l, r, :], rx_d.at[l, r, :]]
+
+    def bring_d(l, half):
+        parts = d_parts(l, half)
+        remote(sxd.at[0, 0], parts[2], xd_s.at[0, 0], xd_r.at[l, half], at_x).wait_recv()
+        for n, part in enumerate(parts):
+            bring(n, part, start)
+
+    def add_d(l, half):
+        add_up(d_parts(l, half), [gd_hbm.at[l, rows(half * DH + RB * n, RB), :] for n in range(2)])
+
+    def other_core_d(l):
         remote(sd, rd_d.at[l], d_s.at[3], d_rd.at[l], at_p).wait_recv()
-        for half in range(2):
-            part = rx_d.at[l, half * DH : (half + 1) * DH, :]
-            remote(sxd.at[0, 0], part, xd_s.at[0, 0], xd_r.at[l, half], at_x).wait_recv()
-        for half in range(2):
-            r = slice(half * DH, (half + 1) * DH)
-            add_up([own_d.at[l, r, :], rd_d.at[l, r, :], rx_d.at[l, r, :]], [(0, DH, gd_hbm.at[l, r, :])])
 
     def backward(l, a, k, t):
         r, slot = tile(t), k % 2
@@ -334,13 +424,9 @@
         acc_gu[...] += dot(a[r, :], dgu_s[...], TN)
         acc_d[...] += dot(act_s[...], do[r, :], TN)
 
-    stage(1, 0, False)
-
     @pl.loop(0, 4)
     def _(k):
-        @pl.when(k > 0)
-        def _():
-            stage(1, k, False)
+        stage(1, k, far_first(k), drain)
 
         @pl.loop(0, T // TM)
         def _(t):
@@ -350,34 +436,40 @@
             def _():
                 across(1, k - 1, False)
 
-            @pl.when((t == 1) & (k == 0))
+            @functools.partial(at, t, 0, k, 0)
             def _():
                 forward_y(1, 2, 3)
-                forward_x(1, 8, 4, 5)
-
-            @pl.when((t == 2) & (k == 0))
-            def _():
+                forward_x(1, 9)
+
+            @functools.partial(at, t, 1, k, 0)
+            def _():
+                forward_y(1, 9)
+                forward_x(1, 4, 5)
+
+            @functools.partial(at, t, 2, k, 0)
+            def _():
+                forward_y(1, 4, 5)
                 forward_x(1, 6, 7)
-                landed(1, 2, 3)
-                stage(1, 1, True)
-
-            @pl.when((t == 1) & (k == 1))
-            def _():
-                forward_y(1, 8, 4, 5, 6, 7)
-
-            @pl.when((t == 2) & (k == 1))
-            def _():
-                landed(1, 8, 4, 5)
-                stage(1, 2, True)
-
-            @pl.when((t == 2) & (k == 2))
+                landed(1, 2, 3, 9)
+                stage(1, 1, far_first(1), start)
+
+            @functools.partial(at, t, 0, k, 1)
+            def _():
+                forward_y(1, 6, 7)
+
+            @functools.partial(at, t, 2, k, 1)
+            def _():
+                landed(1, 4, 5)
+                stage(1, 2, far_first(2), start)
+
+            @functools.partial(at, t, 2, k, 2)
             def _():
                 landed(1, 6, 7)
-                stage(1, 3, True)
-
-            @pl.when((t == 2) & (k == 3))
-            def _():
-                stage(0, 0, True)
+                stage(1, 3, far_first(3), start)
+
+            @functools.partial(at, t, 2, k, 3)
+            def _():
+                stage(0, 0, far_first(0), start)
 
         send_sums(1, k)
 
@@ -393,7 +485,7 @@
 
     @pl.loop(0, 4)
     def _(k):
-        stage(0, k, False)
+        stage(0, k, far_first(k), drain)
 
         @pl.loop(0, T // TM)
         def _(t):
@@ -406,41 +498,68 @@
             @pl.when((t == 0) & (k > 0))
             def _():
                 across(0, k - 1, True)
+                put_done()
+
+            @pl.when(t == 0)
+            def _():
+                bring_gu(1, k)
+
+            @pl.when(t == 1)
+            def _():
+                add_gu(1, k)
 
             @pl.when((t == 2) & (k < 3))
             def _():
-                stage(0, k + 1, True)
-
-            @pl.when(t == 2)
-            def _():
-                finish_gu(1, k)
+                stage(0, k + 1, far_first(k + 1), start)
+
+            @functools.partial(at, t, 2, k, 0)
+            def _():
+                other_core_d(1)
+
+            @pl.when((t == 2) & (k < 2))
+            def _():
+                put_done()
+                bring_d(1, k)
+
+            @pl.when((t == 3) & (k < 2))
+            def _():
+                add_d(1, k)
 
         send_sums(0, k)
 
     across(0, 3, True)
-    finish_d(1)
-
-    @pl.loop(0, 4)
+    other_core_d(0)
+
+    @pl.loop(0, 2)
     def _(k):
-        finish_gu(0, k)
-
-    finish_d(0)
+        put_done()
+        bring_gu(0, k)
+        add_gu(0, k)
+        put_done()
+        bring_d(0, k)
+        add_d(0, k)
+
+    @pl.loop(2, 4)
+    def _(k):
+        put_done()
+        bring_gu(0, k)
+        add_gu(0, k)
 
     part = ssq[:, :128]
     for n in range(1, D // 128):
         part = part + ssq[:, n * 128 : (n + 1) * 128]
     ss_src[...] = part
     for l in range(L):
-        for p in range(9):
+        for p in range(10):
             for which, (src, half, to) in enumerate(((ix, y, at_x), (ix, y, at_y), (ix, y, at_p), (ix, 1 - y, at_p))):
                 if which == 0:
-                    send_x(l, p).wait_send()
+                    send_x(l, p, drain)
                 else:
                     r = mine(l, p, src, half)
                     remote(r, r, ag_s.at[l, p, which], ag_r.at[l, p, which], to).wait_send()
         for m in range(3):
             to_peer(l, m).wait_send()
-        for k in (2, 3):
+        for k in (0, 1):
             xd_copy(l, k).wait_send()
     for k in range(4):
         x_copy(0, k).wait_send()
@@ -453,6 +572,7 @@
         remote(ss_src, ss.at[src], ss_s.at[0], ss_r.at[src], at_x).wait_recv()
     for tell in tells:
         tell.wait_send()
+    put_done()
     ss[i] = part
     total = jnp.sum(ss[0] + ss[1] + ss[2] + ss[3])
     fac[...] = jnp.minimum(1.0, 0.5 * lax.rsqrt(jnp.full((8, 128), total / COUNT + 1e-30, f32)))
@@ -482,7 +602,7 @@
             pltpu.VMEM((2, 2 * RB, C), bf16), pltpu.VMEM((2, DH, D), bf16),
             pltpu.VMEM((4, 2 * RB, C), bf16), pltpu.VMEM((2, 2, DH, D), bf16),
             pltpu.VMEM((8, D), f32), pltpu.VMEM((4, 8, 128), f32), pltpu.VMEM((8, 128), f32),
-            dma(L, 9, 4), dma(L, 9, 4), dma(L, 3), dma(L, 3), dma(2), dma(2, 7),
+            dma(L, 10, 4), dma(L, 10, 4), dma(L, 3), dma(L, 3), dma(2), dma(2, 7),
             dma(4), dma(2), dma(2), dma(L, 4), dma(L), dma(2), dma(4), dma(L, 4), dma(L, 2), dma(L, 2),
             dma(3), dma(2), dma(3), dma(4),
         ],
@@ -508,13 +628,13 @@
 
 
 def adamw(factor, g, w, m, v):
-    wide = pl.BlockSpec((1, RB // 12, FF), lambda t: (t // 12, t % 12, 0))
-    tall = pl.BlockSpec((1, C // 12, D), lambda t: (t // 12, t % 12, 0))
+    wide = pl.BlockSpec((1, RB // N, FF), lambda t: (t // N, t % N, 0))
+    tall = pl.BlockSpec((1, C // N, D), lambda t: (t // N, t % N, 0))
     specs = [wide, wide, tall]
     shapes = lambda dtype: [jax.ShapeDtypeStruct(a.shape, dtype) for a in w]
     return pl.pallas_call(
         adamw_kernel,
-        grid=(24,),
+        grid=(L * N,),
         in_specs=[pl.BlockSpec((8, 128), lambda t: (0, 0))] + specs * 4,
         out_specs=specs * 3,
         out_shape=shapes(bf16) + shapes(f32) + shapes(f32),

time: 348 us -> 313 us (0.90)
  Pallas kernels: 347 us -> 311 us
    pallas_call x1, Pallas kernels: 313 us -> 285 us  [gradients(): pl.pallas_call(step_kernel, in_specs=[hbm] * 5, out_specs=[hbm] * 3 + [vm...]
    pallas_call x1, Pallas kernels: 33.8 us -> 26.4 us  [adamw(): pl.pallas_call(adamw_kernel, grid=(L * N,), in_specs=[pl.BlockSpec((8, 12...]
where the time goes in v2:
time: 313 us; the launch traced here: 312 us
  Pallas kernels  311 us (99%)
    pallas_call x1, Pallas kernels, gradients(): pl.pallas_call(step_kernel, in_specs=[hbm] * 5, out_specs=[hbm] * 3 + [vm...  285 us
    pallas_call x1, Pallas kernels, adamw(): pl.pallas_call(adamw_kernel, grid=(L * N,), in_specs=[pl.BlockSpec((8, 12...  26.4 us

profile of v2, /device:TPU:0, one launch (start us, length us, event | category | flops | bytes accessed | tf_op | source)
XLA Modules:
  0.0 312.2 jit_solution(13306036175345610747)
XLA Ops:
  0.6 285.0 %train_step.1 = (bf16[2,192,3072]{2,1,0:T(8,128)(2,1)}, bf16[2,192,3072]{2,1,0:T(8,128)(2,1)}, bf16[2,768,768]{2,1,0:T(8,128)(2,1)}, f32[8,128]{1,0:T(8,128)}, b...) custom-call(bf16[2048,768]{1,0:T(8,128)(2,1)} %bitcast.2, ...), custom_call_target="tpu_custom_call" | custom-call | tf_op jit(solution)/shard_map/train_step/pallas_call | solution.py:586
  285.6 26.4 %adamw.1 = (bf16[2,192,3072]{2,1,0:T(8,128)(2,1)}, bf16[2,192,3072]{2,1,0:T(8,128)(2,1)}, bf16[2,768,768]{2,1,0:T(8,128)(2,1)}, f32[2,192,3072]{2,1,0:T(8,128)},...) custom-call(f32[8,128]{1,0:T(8,128)} %get-tuple-element.13.refs_0_, ...), custom_call_target="tpu_custom_call" | custom-call | tf_op jit(solution)/shard_map/adamw/pallas_call | solution.py:635

commit v3 on v2

v3 whole, which is shorter than its diff:
```python
import functools

import jax
import jax.numpy as jnp
from jax import lax
from jax.experimental import pallas as pl
from jax.experimental.pallas import tpu as pltpu
from jax.sharding import PartitionSpec as P

T, D, FF, L = 2048, 768, 3072, 2
C = 768
TM = 512
RB = D // 4
RH = RB // 2
DH = C // 2
DQ = C // 4
N = 4
COUNT = 3 * L * D * FF
FIRST, SECOND, THIRD, LAST = range(4)
OVER_X, OVER_Y, TO_CORE, Y_TO_CORE = range(4)
GU = [(n, n + 1) for n in range(0, 8, 2)]
GU_1, GU_2, GU_3, GU_4 = GU
DOWN_1, DOWN_2 = (8,), (9,)
ONE, TWO = range(L)
bf16, f32 = jnp.bfloat16, jnp.float32
NT = (((1,), (1,)), ((), ()))
TN = (((0,), (0,)), ((), ()))
MESH = pl.DeviceIdType.MESH


def dot(a, b, dims=(((1,), (0,)), ((), ()))):
    return lax.dot_general(a, b, dims, preferred_element_type=f32)


def scale_of(wide):
    return lax.rsqrt(jnp.mean(wide * wide, -1, keepdims=True) + 1e-6)


def step_kernel(
    x_hbm, dy_hbm, wg, wu, wd,
    gg_hbm, gu_hbm, gd_hbm, fac, all_g, all_u, all_d, p0_hbm, rd2_hbm, rx_hbm, own_d, rd_d, rx_d, up_hbm, act_hbm,
    h, a0, a1, do, acc, acc_gu, acc_d, w_gu, w_d, act_s, dgu_s, sg, sd, rd3, rd3d, sx, sxd, ssq, ss, ss_src, up_s,
    ag_s, ag_r, pe_s, pe_r, ld, wsem, d_s, d_r3, dd_s, d_r3d, d_r2, d_rd, keep, x_s, x_r, xd_s, xd_r, fsem, fout, ss_s, ss_r, save, back,
):
    y, i = lax.axis_index("rep"), lax.axis_index("dp")
    xx, c = i // 2, i % 2
    ix, ip, iq = (1 - xx) * 2 + c, xx * 2 + 1 - c, (1 - xx) * 2 + 1 - c
    at_x, at_p, at_q, at_y = (y, ix), (y, ip), (y, iq), (1 - y, i)

    def remote(src, dst, send, recv, to):
        return pltpu.make_async_remote_copy(
            src_ref=src, dst_ref=dst, send_sem=send, recv_sem=recv, device_id=to, device_id_type=MESH
        )

    def near_first(k):
        return (2 * xx + k) % 4

    def far_first(k):
        return (2 * (1 - xx) + k) % 4

    def far_between(k, side=xx):
        return 2 * ((side + (k + 1) // 2) % 2) + k // 2

    def start(copy):
        copy.start()

    def drain(copy):
        copy.wait_send() if copy.is_remote else copy.wait()

    def at(t, n, k, m):
        return pl.when((t == n) & (k == m))

    def cols(j):
        return pl.ds(pl.multiple_of(j * C, C), C)

    def rows(start, size):
        return pl.ds(pl.multiple_of(start, 32), size)

    barrier = pltpu.get_barrier_semaphore()
    for other in (at_x, at_p, at_q, at_y):
        pl.semaphore_signal(barrier, inc=1, device_id=other, device_id_type=MESH)
    load_x = pltpu.make_async_copy(x_hbm, h, ld.at[0])
    load_dy = pltpu.make_async_copy(dy_hbm, do, ld.at[1])
    load_x.start()
    load_dy.start()
    pl.semaphore_wait(barrier, 4)

    def region(l, p, src, half, j):
        if p >= 8:
            return all_d.at[l, rows(C * (src // 2 * 2 + p - 8) + DH * half + DQ * (src % 2), DQ), :]
        return (all_g, all_u)[p % 2].at[l, rows(RB * src + RH * half, RH), cols(j)]

    def mine(l, p, src, half):
        return region(l, p, src, half, (near_first, far_between)[l](p // 2))

    def send_x(l, p, act):
        j = far_between(p // 2, 1 - xx) if l else far_first(p // 2)
        there = region(l, p, i, y, j)

        def copy(src):
            return remote(src, there, ag_s.at[l, p, OVER_X], ag_r.at[l, p, OVER_X], at_x)

        if p < 8:
            act(copy((wg, wu)[p % 2].at[l, rows(RH * y, RH), cols(j)]))
        elif act is start:

            @pl.when(c == p - 8)
            def _():
                act(copy(wd.at[l, rows(DH * y + DQ * c, DQ), :]))

            @pl.when(c != p - 8)
            def _():
                act(copy(there))
        else:
            act(copy(there))

    def forward_x(l, *pieces):
        for p in sum(pieces, ()):
            r = mine(l, p, ix, y)
            remote(r, r, ag_s.at[l, p, OVER_X], ag_r.at[l, p, OVER_X], at_x).wait_recv()
            remote(r, r, ag_s.at[l, p, OVER_Y], ag_r.at[l, p, OVER_Y], at_y).start()
            remote(r, r, ag_s.at[l, p, TO_CORE], ag_r.at[l, p, TO_CORE], at_p).start()

    def forward_y(l, *pieces):
        for p in sum(pieces, ()):
            r = mine(l, p, ix, 1 - y)
            remote(r, r, ag_s.at[l, p, OVER_Y], ag_r.at[l, p, OVER_Y], at_y).wait_recv()
            remote(r, r, ag_s.at[l, p, Y_TO_CORE], ag_r.at[l, p, Y_TO_CORE], at_p).start()

    def landed(l, *pieces):
        for p in sum(pieces, ()):
            for which, half in ((TO_CORE, y), (Y_TO_CORE, 1 - y)):
                r = mine(l, p, iq, half)
                remote(r, r, ag_s.at[l, p, which], ag_r.at[l, p, which], at_p).wait_recv()

    def to_peer(l, m):
        src = (wg, wu, wd)[m].at[l]
        dst = (all_g.at[l, rows(RB * i, RB), :], all_u.at[l, rows(RB * i, RB), :], all_d.at[l, rows(C * i, C), :])[m]
        return remote(src, dst, pe_s.at[l, m], pe_r.at[l, m], at_p)

    def from_peer(l):
        for m in range(3):
            to_peer(l, m).wait_recv()

    def send(l, *pieces):
        for p in sum(pieces, ()):
            send_x(l, p, start)

    send(ONE, GU_1, GU_2, GU_3)
    for l in range(L):
        for m in range(3):
            to_peer(l, m).start()

    def stage_gu(l, k, j, act):
        slot = k % 2
        for m, (own, gathered) in enumerate(((wg, all_g), (wu, all_u))):
            for n, (src, row, size) in enumerate(
                (
                    (own.at[l, :, cols(j)], RB * i, RB),
                    (gathered.at[l, rows(RB * ip, RB), cols(j)], RB * ip, RB),
                    (gathered.at[l, rows(2 * RB * (1 - xx), 2 * RB), cols(j)], 2 * RB * (1 - xx), 2 * RB),
                )
            ):
                copy = pltpu.make_async_copy(
                    src, w_gu.at[slot, rows(row, size), m * C : (m + 1) * C], wsem.at[slot, 3 * m + n]
                )
                act(copy)

    def stage_d(l, k, j, act):
        slot = k % 2
        theirs = pltpu.make_async_copy(all_d.at[l, rows(C * j, C), :], w_d.at[slot], wsem.at[slot, 6])
        if act is start:

            @pl.when(j == i)
            def _():
                pltpu.make_async_copy(wd.at[l], w_d.at[slot], wsem.at[slot, 6]).start()

            @pl.when(j != i)
            def _():
                theirs.start()
        else:
            act(theirs)

    def stage(l, k, j, act):
        stage_gu(l, k, j, act)
        stage_d(l, k, j, act)

    def tile(t):
        return pl.ds(pl.multiple_of(t * TM, TM), TM)

    def clear(ref, size):
        n = ref.shape[0] // size

        @pl.loop(0, n)
        def _(t):
            ref[pl.ds(pl.multiple_of(t * size, size), size), :] = jnp.zeros((size, ref.shape[1]), ref.dtype)

    clear(acc, 256)
    clear(acc_gu, 128)
    clear(acc_d, 128)
    ssq[...] = jnp.zeros_like(ssq)
    load_x.wait()

    @pl.loop(0, T // 256)
    def _(t):
        r = pl.ds(pl.multiple_of(t * 256, 256), 256)
        wide = h[r, :].astype(f32)
        a0[r, :] = (wide * scale_of(wide)).astype(bf16)

    def saving(j, t, act):
        s = t % 2
        act(pltpu.make_async_copy(up_s.at[s], up_hbm.at[j, tile(t), :], save.at[0, s]))
        act(pltpu.make_async_copy(dgu_s.at[:, cols(s)], act_hbm.at[j, tile(t), :], save.at[1, s]))

    def forward(k, t):
        r, s = tile(t), t % 2

        @pl.when((k > 0) | (t > 1))
        def _():
            saving(near_first(k), t, drain)

        gu = dot(a0[r, :], w_gu[k % 2])
        up_s[s] = gu
        gate, up = gu[:, :C], gu[:, C:]
        act = (gate * jax.nn.sigmoid(gate) * up).astype(bf16)
        dgu_s[:, cols(s)] = act
        saving(near_first(k), t, start)
        acc[r, :] += dot(act, w_d[k % 2])

    forward_x(ONE, GU_1)
    from_peer(ONE)
    send(ONE, DOWN_1, GU_4, DOWN_2)
    forward_x(ONE, GU_2)
    forward_y(ONE, GU_1)
    landed(ONE, GU_1)
    stage(ONE, FIRST, near_first(FIRST), start)

    @pl.loop(0, 4)
    def _(k):
        stage(ONE, k, near_first(k), drain)

        @pl.loop(0, T // TM)
        def _(t):
            forward(k, t)

            @at(t, FIRST, k, FIRST)
            def _():
                forward_y(ONE, GU_2)
                forward_x(ONE, GU_3)

            @at(t, SECOND, k, FIRST)
            def _():
                from_peer(TWO)
                send(TWO, GU_1, GU_2, DOWN_1, GU_3, DOWN_2, GU_4)

            @at(t, THIRD, k, FIRST)
            def _():
                landed(ONE, GU_2)
                stage(ONE, SECOND, near_first(SECOND), start)

            @at(t, LAST, k, FIRST)
            def _():
                forward_x(ONE, DOWN_1)
                forward_y(ONE, GU_3)

            @at(t, SECOND, k, SECOND)
            def _():
                landed(ONE, GU_3)
                stage_gu(ONE, THIRD, near_first(THIRD), start)

            @at(t, THIRD, k, SECOND)
            def _():
                forward_x(ONE, GU_4)
                forward_y(ONE, DOWN_1)

            @at(t, LAST, k, SECOND)
            def _():
                landed(ONE, DOWN_1)
                stage_d(ONE, THIRD, near_first(THIRD), start)

            @at(t, FIRST, k, THIRD)
            def _():
                forward_x(ONE, DOWN_2)
                forward_y(ONE, GU_4)

            @at(t, THIRD, k, THIRD)
            def _():
                landed(ONE, GU_4)
                stage_gu(ONE, LAST, near_first(LAST), start)
                forward_x(TWO, GU_1)

            @at(t, LAST, k, THIRD)
            def _():
                forward_y(ONE, DOWN_2)
                landed(ONE, DOWN_2)
                stage_d(ONE, LAST, near_first(LAST), start)

            @at(t, FIRST, k, LAST)
            def _():
                forward_x(TWO, GU_2)
                forward_y(TWO, GU_1)

            @at(t, THIRD, k, LAST)
            def _():
                forward_x(TWO, DOWN_1)
                forward_y(TWO, GU_2)
                landed(TWO, GU_1)
                stage(TWO, FIRST, far_between(FIRST), start)

    for n in (THIRD, LAST):
        saving(near_first(LAST), n, drain)
    load_dy.wait()

    @pl.loop(0, T // 256)
    def _(t):
        r = pl.ds(pl.multiple_of(t * 256, 256), 256)
        wide = (h[r, :].astype(f32) + acc[r, :].astype(bf16).astype(f32)).astype(bf16)
        h[r, :] = wide
        wide = wide.astype(f32)
        a1[r, :] = (wide * scale_of(wide)).astype(bf16)
        acc[r, :] = jnp.zeros((256, D), f32)

    def gu_copies(l, k, j, act):
        act(remote(sg.at[3], rd3.at[k % 2], d_s.at[0], d_r3.at[k % 2], at_p))
        act(remote(sg.at[2], rd2_hbm.at[l, j], d_s.at[1], d_r2.at[l, j], at_p))
        act(pltpu.make_async_copy(sg.at[0], p0_hbm.at[l, j], keep.at[0]))

    def far_copy(q):
        return remote(sd.at[q, rows(DH * (1 - c), DH), :], rd3d.at[q], dd_s.at[0, q], d_r3d.at[q], at_p)

    def near_copy(l, q, act):
        @pl.when(c != q)
        def _():
            act(remote(sd.at[q], rd_d.at[l], dd_s.at[1, q], d_rd.at[l], at_p))

        @pl.when(c == q)
        def _():
            act(pltpu.make_async_copy(sd.at[q], own_d.at[l], keep.at[1]))

    def round_gu():
        for r, dest in ((3, iq), (1, ix), (2, ip), (0, i)):
            for m in range(2):
                sg[r, RB * m : RB * (m + 1), :] = acc_gu[rows(RB * dest, RB), m * C : (m + 1) * C].astype(bf16)
        clear(acc_gu, 128)

    def round_d(q):
        sd[q] = acc_d[...].astype(bf16)
        clear(acc_d, 128)

    def x_copy(l, k, j):
        return remote(sx.at[k], rx_hbm.at[l, j], x_s.at[k], x_r.at[l, j], at_x)

    def xd_copy(l, q):
        return remote(sxd.at[l, q], rx_d.at[l, rows(DH * c, DH), :], xd_s.at[l, q], xd_r.at[l, c], (y, 2 * (1 - xx) + q))

    def gu_across(l, k, j):
        remote(sg.at[3], rd3.at[k % 2], d_s.at[0], d_r3.at[k % 2], at_p).wait_recv()
        if l == ONE:
            x_copy(l, k, j).wait_send()
        sx[k] = (sg[1].astype(f32) + rd3[k % 2].astype(f32)).astype(bf16)
        x_copy(l, k, j).start()
        gu_copies(l, k, j, drain)

    def d_across(l, q):
        far_copy(q).wait_recv()
        sxd[l, q] = (sd[q, rows(DH * c, DH), :].astype(f32) + rd3d[q].astype(f32)).astype(bf16)
        xd_copy(l, q).start()
        drain(far_copy(q))

    def bring(n, part, act):
        act(pltpu.make_async_copy(part, h.at[n * 384 : (n + 1) * 384, :], fsem.at[n]))

    def put(n, dst, act):
        act(pltpu.make_async_copy(h.at[1152 + RB * n : 1152 + RB * (n + 1), :], dst, fout.at[n]))

    def add_up(parts, puts):
        for n, part in enumerate(parts):
            bring(n, part, drain)
        for r in range(0, 384, 128):
            g = h[r : r + 128, :].astype(f32) + h[384 + r : 512 + r, :].astype(f32) + h[768 + r : 896 + r, :].astype(f32)
            g = g.astype(bf16)
            h[1152 + r : 1280 + r, :] = g
            g = g.astype(f32)
            ssq[...] += jnp.sum((g * g).reshape(16, 8, D), axis=0)
        for n, dst in enumerate(puts):
            put(n, dst, start)

    def put_done():
        for n in range(2):
            put(n, gg_hbm.at[0, :, 0:C], drain)

    def arrival(l, k):
        return near_first(k) if l == ONE else far_between(k, 1 - xx)

    def gu_parts(l, k):
        j = arrival(l, k)
        return [p0_hbm.at[l, j], rd2_hbm.at[l, j], rx_hbm.at[l, j]]

    def bring_gu(l, k):
        j = arrival(l, k)
        parts = gu_parts(l, k)
        remote(sg.at[2], parts[1], d_s.at[1], d_r2.at[l, j], at_p).wait_recv()
        bring(0, parts[0], start)
        bring(1, parts[1], start)
        remote(sx.at[0], parts[2], x_s.at[0], x_r.at[l, j], at_x).wait_recv()
        bring(2, parts[2], start)

    def add_gu(l, k):
        j = arrival(l, k)
        add_up(gu_parts(l, k), [gg_hbm.at[l, :, cols(j)], gu_hbm.at[l, :, cols(j)]])

    def d_parts(l, half):
        r = rows(half * DH, DH)
        return [own_d.at[l, r, :], rd_d.at[l, r, :], rx_d.at[l, r, :]]

    def bring_d(l, half):
        parts = d_parts(l, half)
        remote(sxd.at[0, 0], parts[2], xd_s.at[0, 0], xd_r.at[l, half], at_x).wait_recv()
        for n, part in enumerate(parts):
            bring(n, part, start)

    def add_d(l, half):
        add_up(d_parts(l, half), [gd_hbm.at[l, rows(half * DH + RB * n, RB), :] for n in range(2)])

    def other_core_d(l):
        remote(sd.at[0], rd_d.at[l], dd_s.at[1, 0], d_rd.at[l], at_p).wait_recv()

    def through(gate, up, dact):
        dact = dact.astype(bf16).astype(f32)
        sig = jax.nn.sigmoid(gate)
        silu = gate * sig
        dgu_s[:, C:] = (dact * silu).astype(bf16)
        dgu_s[:, :C] = (dact * up * (sig + silu * (1.0 - sig))).astype(bf16)
        return (silu * up).astype(bf16)

    def backward_2(k, t):
        r, s = tile(t), k % 2
        gu = dot(a1[r, :], w_gu[s])
        act_s[...] = through(gu[:, :C], gu[:, C:], dot(do[r, :], w_d[s], NT))
        acc[r, :] += dot(dgu_s[...], w_gu[s], NT)
        acc_gu[...] += dot(a1[r, :], dgu_s[...], TN)
        acc_d[...] += dot(act_s[...], do[r, :], TN)

    def saved(j, t):
        return pltpu.make_async_copy(up_hbm.at[j, tile(t), :], up_s.at[t % 2], back.at[t % 2])

    def backward_1(k, t):
        r, s = tile(t), t % 2
        saved(far_first(k), t).wait()

        @pl.when(t < LAST)
        def _():
            saved(far_first(k), t + 1).start()

        @pl.when((t == LAST) & (k < LAST))
        def _():
            saved(far_first(k + 1), FIRST).start()

        through(up_s[s, :, :C], up_s[s, :, C:], dot(do[r, :], w_d[k % 2], NT))
        acc_gu[...] += dot(a0[r, :], dgu_s[...], TN)

    @pl.loop(0, 4)
    def _(k):
        stage(TWO, k, far_between(k), drain)
        far = (k == SECOND) | (k == THIRD)

        @pl.loop(0, T // TM)
        def _(t):
            backward_2(k, t)

            @pl.when((t == FIRST) & (k > FIRST))
            def _():
                gu_across(TWO, k - 1, far_between(k - 1))

            @pl.when((t == FIRST) & ((k == THIRD) | (k == LAST)))
            def _():
                d_across(TWO, k // 2 + k % 2 - 1)

            @at(t, FIRST, k, SECOND)
            def _():
                near_copy(TWO, 0, drain)

            @at(t, FIRST, k, FIRST)
            def _():
                forward_x(TWO, GU_3)
                forward_y(TWO, DOWN_1)

            @at(t, SECOND, k, FIRST)
            def _():
                forward_x(TWO, DOWN_2)
                forward_y(TWO, GU_3)

            @at(t, THIRD, k, FIRST)
            def _():
                forward_x(TWO, GU_4)
                forward_y(TWO, DOWN_2)
                landed(TWO, GU_2, DOWN_1)
                stage(TWO, SECOND, far_between(SECOND), start)

            @at(t, FIRST, k, SECOND)
            def _():
                forward_y(TWO, GU_4)

            @at(t, THIRD, k, SECOND)
            def _():
                landed(TWO, GU_3, DOWN_2)
                stage(TWO, THIRD, far_between(THIRD), start)

            @at(t, THIRD, k, THIRD)
            def _():
                landed(TWO, GU_4)
                stage(TWO, LAST, far_between(LAST), start)

            @at(t, THIRD, k, LAST)
            def _():
                stage_d(ONE, FIRST, far_first(FIRST), start)

        round_gu()
        round_d(k // 2)
        gu_copies(TWO, k, far_between(k), start)

        @pl.when(far)
        def _():
            far_copy(k // 2).start()

        @pl.when(jnp.logical_not(far))
        def _():
            near_copy(TWO, k // 2, start)

    def product(j, to):
        return pltpu.make_async_copy(act_hbm.at[j], to, ld.at[0])

    product(far_first(FIRST), a1).start()
    saved(far_first(FIRST), FIRST).start()

    @pl.loop(0, T // 256)
    def _(t):
        r = pl.ds(pl.multiple_of(t * 256, 256), 256)
        wide = h[r, :].astype(f32)
        scale = scale_of(wide)
        da = acc[r, :].astype(bf16).astype(f32)
        mix = jnp.sum(da * wide, -1, keepdims=True) * (scale * scale * scale / D)
        down = (da * scale - wide * mix).astype(bf16)
        do[r, :] = (do[r, :].astype(f32) + down.astype(f32)).astype(bf16)

    gu_across(TWO, LAST, far_between(LAST))
    near_copy(TWO, 1, drain)

    def down_grad(k, of, then, then_of):
        product(far_first(k), of).wait()
        if then is not None:
            product(far_first(then), then_of).start()

        @pl.loop(0, T // TM)
        def _(t):
            acc_d[...] += dot(of[tile(t), :], do[tile(t), :], TN)

    down_grad(FIRST, a1, SECOND, h)
    round_d(0)
    far_copy(0).start()
    down_grad(SECOND, h, THIRD, a1)
    d_across(ONE, 0)
    round_d(1)
    far_copy(1).start()
    down_grad(THIRD, a1, LAST, h)
    d_across(ONE, 1)
    round_d(0)
    near_copy(ONE, 0, start)
    down_grad(LAST, h, None, None)
    near_copy(ONE, 0, drain)
    round_d(1)
    near_copy(ONE, 1, start)

    @pl.loop(0, 4)
    def _(k):
        stage_d(ONE, k, far_first(k), drain)

        @pl.loop(0, T // TM)
        def _(t):
            backward_1(k, t)

            @at(t, FIRST, k, FIRST)
            def _():
                near_copy(ONE, 1, drain)
                other_core_d(TWO)

            @pl.when((t == FIRST) & ((k == SECOND) | (k == THIRD)))
            def _():
                add_d(TWO, k - 1)

            @pl.when((t == FIRST) & (k > FIRST))
            def _():
                put_done()

            @pl.when(t == FIRST)
            def _():
                bring_gu(TWO, k)

            @pl.when((t == SECOND) & (k > FIRST))
            def _():
                gu_across(ONE, k - 1, far_first(k - 1))

            @pl.when((t == SECOND) & (k < LAST))
            def _():
                stage_d(ONE, k + 1, far_first(k + 1), start)

            @pl.when(t == THIRD)
            def _():
                add_gu(TWO, k)

            @pl.when((t == LAST) & (k < THIRD))
            def _():
                put_done()
                bring_d(TWO, k)

        round_gu()
        gu_copies(ONE, k, far_first(k), start)

    gu_across(ONE, LAST, far_first(LAST))
    other_core_d(ONE)

    @pl.loop(0, 2)
    def _(half):
        put_done()
        bring_d(ONE, half)
        add_d(ONE, half)

    @pl.loop(0, 4)
    def _(k):
        put_done()
        bring_gu(ONE, k)
        add_gu(ONE, k)

    part = ssq[:, :128]
    for n in range(1, D // 128):
        part = part + ssq[:, n * 128 : (n + 1) * 128]
    ss_src[...] = part
    for l in range(L):
        for p in range(10):
            for which, (src, half, to) in enumerate(((ix, y, at_x), (ix, y, at_y), (ix, y, at_p), (ix, 1 - y, at_p))):
                if which == OVER_X:
                    send_x(l, p, drain)
                else:
                    r = mine(l, p, src, half)
                    remote(r, r, ag_s.at[l, p, which], ag_r.at[l, p, which], to).wait_send()
        for m in range(3):
            to_peer(l, m).wait_send()
        for q in range(2):
            xd_copy(l, q).wait_send()
    for k in range(4):
        x_copy(ONE, k, far_first(k)).wait_send()
    tells = [
        remote(ss_src, ss.at[i], ss_s.at[n], ss_r.at[i], to) for n, to in enumerate((at_x, at_p, at_q))
    ]
    for tell in tells:
        tell.start()
    for src in (ix, ip, iq):
        remote(ss_src, ss.at[src], ss_s.at[0], ss_r.at[src], at_x).wait_recv()
    for tell in tells:
        tell.wait_send()
    put_done()
    ss[i] = part
    total = jnp.sum(ss[0] + ss[1] + ss[2] + ss[3])
    fac[...] = jnp.minimum(1.0, 0.5 * lax.rsqrt(jnp.full((8, 128), total / COUNT + 1e-30, f32)))


def gradients(x, dy, wg, wu, wd):
    hbm = pl.BlockSpec(memory_space=pl.ANY)
    vmem = pl.BlockSpec(memory_space=pltpu.VMEM)
    out = lambda *shape: jax.ShapeDtypeStruct(shape, bf16)
    dma = lambda *shape: pltpu.SemaphoreType.DMA(shape)
    return pl.pallas_call(
        step_kernel,
        in_specs=[hbm] * 5,
        out_specs=[hbm] * 3 + [vmem] + [hbm] * 11,
        out_shape=[
            out(L, RB, FF), out(L, RB, FF), out(L, C, D), jax.ShapeDtypeStruct((8, 128), f32),
            out(L, D, FF), out(L, D, FF), out(L, FF, D),
            out(L, 4, 2 * RB, C), out(L, 4, 2 * RB, C), out(L, 4, 2 * RB, C),
            out(L, C, D), out(L, C, D), out(L, C, D),
            jax.ShapeDtypeStruct((4, T, 2 * C), f32), out(4, T, C),
        ],
        scratch_shapes=[
            pltpu.VMEM((T, D), bf16), pltpu.VMEM((T, D), bf16), pltpu.VMEM((T, D), bf16), pltpu.VMEM((T, D), bf16),
            pltpu.VMEM((T, D), f32), pltpu.VMEM((D, 2 * C), f32), pltpu.VMEM((C, D), f32),
            pltpu.VMEM((2, D, 2 * C), bf16), pltpu.VMEM((2, C, D), bf16),
            pltpu.VMEM((TM, C), bf16), pltpu.VMEM((TM, 2 * C), bf16),
            pltpu.VMEM((4, 2 * RB, C), bf16), pltpu.VMEM((2, C, D), bf16),
            pltpu.VMEM((2, 2 * RB, C), bf16), pltpu.VMEM((2, DH, D), bf16),
            pltpu.VMEM((4, 2 * RB, C), bf16), pltpu.VMEM((2, 2, DH, D), bf16),
            pltpu.VMEM((8, D), f32), pltpu.VMEM((4, 8, 128), f32), pltpu.VMEM((8, 128), f32), pltpu.VMEM((2, TM, 2 * C), f32),
            dma(L, 10, 4), dma(L, 10, 4), dma(L, 3), dma(L, 3), dma(2), dma(2, 7),
            dma(2), dma(2), dma(2, 2), dma(2), dma(L, 4), dma(L), dma(2), dma(4), dma(L, 4), dma(L, 2), dma(L, 2),
            dma(3), dma(2), dma(3), dma(4), dma(2, 2), dma(2),
        ],
        compiler_params=pltpu.CompilerParams(
            collective_id=0, has_side_effects=True, vmem_limit_bytes=63 * 2**20
        ),
        name="train_step",
    )(x, dy, wg, wu, wd)


def adamw_kernel(*refs):
    fac, ins, outs = refs[0], refs[1:13], refs[13:]
    factor = fac[0:1, 0:1]
    for n in range(3):
        g, w, m, v = (ins[3 * which + n] for which in range(4))
        grad = g[0].astype(f32) * factor
        new_m = 0.9 * m[0] + 0.1 * grad
        new_v = 0.95 * v[0] + 0.05 * grad * grad
        wide = w[0].astype(f32)
        outs[n][0] = (wide - 0.02 * (new_m * lax.rsqrt(new_v + 1e-8) + 0.1 * wide)).astype(bf16)
        outs[3 + n][0] = new_m
        outs[6 + n][0] = new_v


def adamw(factor, g, w, m, v):
    wide = pl.BlockSpec((1, RB // N, FF), lambda t: (t // N, t % N, 0))
    tall = pl.BlockSpec((1, C // N, D), lambda t: (t // N, t % N, 0))
    specs = [wide, wide, tall]
    shapes = lambda dtype: [jax.ShapeDtypeStruct(a.shape, dtype) for a in w]
    return pl.pallas_call(
        adamw_kernel,
        grid=(L * N,),
        in_specs=[pl.BlockSpec((8, 128), lambda t: (0, 0))] + specs * 4,
        out_specs=specs * 3,
        out_shape=shapes(bf16) + shapes(f32) + shapes(f32),
        compiler_params=pltpu.CompilerParams(vmem_limit_bytes=63 * 2**20),
        name="adamw",
    )(factor, *g, *w, *m, *v)


def solution(mesh):
    def step(x, dy, *arrays):
        w, m, v = (arrays[n : n + 3] for n in (0, 3, 6))
        gg, gu, gd, factor, *_ = gradients(x[0], dy[0], *w)
        return tuple(adamw(factor, (gg, gu, gd), w, m, v))

    states, cut = P(("rep", "dp"), None, None), P(None, "dp", None)
    return jax.shard_map(
        step,
        mesh=mesh,
        in_specs=(states, states) + (cut,) * 9,
        out_specs=(P("rep", "dp", None),) * 9,
        check_vma=False,
    )
```

time: 313 us -> 305 us (0.974)
  Pallas kernels: 311 us -> 304 us
    pallas_call x1, Pallas kernels: 285 us -> 277 us  [gradients(): pl.pallas_call(step_kernel, in_specs=[hbm] * 5, out_specs=[hbm] * 3 + [vm...]
where the time goes in v3:
time: 305 us; the launch traced here: 304 us
  Pallas kernels  304 us (100%)
    pallas_call x1, Pallas kernels, gradients(): pl.pallas_call(step_kernel, in_specs=[hbm] * 5, out_specs=[hbm] * 3 + [vm...  277 us
    pallas_call x1, Pallas kernels, adamw(): pl.pallas_call(adamw_kernel, grid=(L * N,), in_specs=[pl.BlockSpec((8, 12...  26.4 us

profile of v3, /device:TPU:0, one launch (start us, length us, event | category | flops | bytes accessed | tf_op | source)
XLA Modules:
  0.0 304.4 jit_solution(7431346990790858493)
XLA Ops:
  0.6 277.2 %train_step.1 = (bf16[2,192,3072]{2,1,0:T(8,128)(2,1)}, bf16[2,192,3072]{2,1,0:T(8,128)(2,1)}, bf16[2,768,768]{2,1,0:T(8,128)(2,1)}, f32[8,128]{1,0:T(8,128)}, b...) custom-call(bf16[2048,768]{1,0:T(8,128)(2,1)} %bitcast.2, ...), custom_call_target="tpu_custom_call" | custom-call | tf_op jit(solution)/shard_map/train_step/pallas_call | solution.py:672
  277.8 26.4 %adamw.1 = (bf16[2,192,3072]{2,1,0:T(8,128)(2,1)}, bf16[2,192,3072]{2,1,0:T(8,128)(2,1)}, bf16[2,768,768]{2,1,0:T(8,128)(2,1)}, f32[2,192,3072]{2,1,0:T(8,128)},...) custom-call(f32[8,128]{1,0:T(8,128)} %get-tuple-element.13.refs_0_, ...), custom_call_target="tpu_custom_call" | custom-call | tf_op jit(solution)/shard_map/adamw/pallas_call | solution.py:722

commit v4 on v3

--- a/solution.py
+++ b/solution.py
@@ -58,17 +58,24 @@
     def far_first(k):
         return (2 * (1 - xx) + k) % 4
 
-    def far_between(k, side=xx):
-        return 2 * ((side + (k + 1) // 2) % 2) + k // 2
-
     def start(copy):
         copy.start()
 
     def drain(copy):
         copy.wait_send() if copy.is_remote else copy.wait()
 
-    def at(t, n, k, m):
-        return pl.when((t == n) & (k == m))
+    def duties(t, k, *work):
+        for n in range(T // TM):
+            here = [(m, f) for tile_n, m, f in work if tile_n == n]
+            if here:
+
+                @pl.when(t == n)
+                def _():
+                    for m, f in here:
+                        if m is None:
+                            f()
+                        else:
+                            pl.when(k == m)(f)
 
     def cols(j):
         return pl.ds(pl.multiple_of(j * C, C), C)
@@ -91,10 +98,10 @@
         return (all_g, all_u)[p % 2].at[l, rows(RB * src + RH * half, RH), cols(j)]
 
     def mine(l, p, src, half):
-        return region(l, p, src, half, (near_first, far_between)[l](p // 2))
+        return region(l, p, src, half, (near_first, far_first)[l](p // 2))
 
     def send_x(l, p, act):
-        j = far_between(p // 2, 1 - xx) if l else far_first(p // 2)
+        j = (far_first, near_first)[l](p // 2)
         there = region(l, p, i, y, j)
 
         def copy(src):
@@ -235,6 +242,35 @@
     landed(ONE, GU_1)
     stage(ONE, FIRST, near_first(FIRST), start)
 
+    def begin():
+        from_peer(TWO)
+        send(TWO, GU_1, DOWN_1, GU_2, DOWN_2, GU_3, GU_4)
+        forward_x(ONE, GU_3[:1])
+
+    def ready_gu(l, k, j, *pieces):
+        landed(l, *pieces)
+        stage_gu(l, k, j, start)
+
+    def ready_d(l, k, j, *pieces):
+        landed(l, *pieces)
+        stage_d(l, k, j, start)
+
+    def ready(l, k, j, *pieces):
+        landed(l, *pieces)
+        stage(l, k, j, start)
+
+    def later(f, *args):
+        return lambda: f(*args)
+
+    def pass_later(*args):
+        def go():
+            for f, *rest in args:
+                f(*rest)
+
+        return go
+
+    X, Y = forward_x, forward_y
+
     @pl.loop(0, 4)
     def _(k):
         stage(ONE, k, near_first(k), drain)
@@ -242,74 +278,30 @@
         @pl.loop(0, T // TM)
         def _(t):
             forward(k, t)
-
-            @at(t, FIRST, k, FIRST)
-            def _():
-                forward_y(ONE, GU_2)
-                forward_x(ONE, GU_3)
-
-            @at(t, SECOND, k, FIRST)
-            def _():
-                from_peer(TWO)
-                send(TWO, GU_1, GU_2, DOWN_1, GU_3, DOWN_2, GU_4)
-
-            @at(t, THIRD, k, FIRST)
-            def _():
-                landed(ONE, GU_2)
-                stage(ONE, SECOND, near_first(SECOND), start)
-
-            @at(t, LAST, k, FIRST)
-            def _():
-                forward_x(ONE, DOWN_1)
-                forward_y(ONE, GU_3)
-
-            @at(t, SECOND, k, SECOND)
-            def _():
-                landed(ONE, GU_3)
-                stage_gu(ONE, THIRD, near_first(THIRD), start)
-
-            @at(t, THIRD, k, SECOND)
-            def _():
-                forward_x(ONE, GU_4)
-                forward_y(ONE, DOWN_1)
-
-            @at(t, LAST, k, SECOND)
-            def _():
-                landed(ONE, DOWN_1)
-                stage_d(ONE, THIRD, near_first(THIRD), start)
-
-            @at(t, FIRST, k, THIRD)
-            def _():
-                forward_x(ONE, DOWN_2)
-                forward_y(ONE, GU_4)
-
-            @at(t, THIRD, k, THIRD)
-            def _():
-                landed(ONE, GU_4)
-                stage_gu(ONE, LAST, near_first(LAST), start)
-                forward_x(TWO, GU_1)
-
-            @at(t, LAST, k, THIRD)
-            def _():
-                forward_y(ONE, DOWN_2)
-                landed(ONE, DOWN_2)
-                stage_d(ONE, LAST, near_first(LAST), start)
-
-            @at(t, FIRST, k, LAST)
-            def _():
-                forward_x(TWO, GU_2)
-                forward_y(TWO, GU_1)
-
-            @at(t, THIRD, k, LAST)
-            def _():
-                forward_x(TWO, DOWN_1)
-                forward_y(TWO, GU_2)
-                landed(TWO, GU_1)
-                stage(TWO, FIRST, far_between(FIRST), start)
-
+            duties(
+                t, k,
+                (FIRST, FIRST, begin),
+                (SECOND, FIRST, pass_later((X, ONE, GU_3[1:]), (Y, ONE, GU_2))),
+                (THIRD, FIRST, later(ready, ONE, SECOND, near_first(SECOND), GU_2)),
+                (FIRST, SECOND, pass_later((X, ONE, DOWN_1), (Y, ONE, GU_3))),
+                (SECOND, SECOND, pass_later((X, ONE, GU_4[:1]))),
+                (SECOND, SECOND, later(ready_gu, ONE, THIRD, near_first(THIRD), GU_3)),
+                (THIRD, SECOND, pass_later((X, ONE, GU_4[1:]), (Y, ONE, DOWN_1))),
+                (LAST, SECOND, later(ready_d, ONE, THIRD, near_first(THIRD), DOWN_1)),
+                (FIRST, THIRD, pass_later((X, ONE, DOWN_2), (Y, ONE, GU_4))),
+                (SECOND, THIRD, later(ready_gu, ONE, LAST, near_first(LAST), GU_4)),
+                (THIRD, THIRD, pass_later((X, TWO, GU_1[:1]))),
+                (LAST, THIRD, pass_later((X, TWO, GU_1[1:]), (Y, ONE, DOWN_2))),
+                (LAST, THIRD, later(ready_d, ONE, LAST, near_first(LAST), DOWN_2)),
+                (FIRST, LAST, pass_later((X, TWO, DOWN_1), (Y, TWO, GU_1))),
+                (SECOND, LAST, later(ready_gu, TWO, FIRST, far_first(FIRST), GU_1)),
+                (THIRD, LAST, pass_later((X, TWO, GU_2[:1]))),
+                (LAST, LAST, pass_later((X, TWO, GU_2[1:]), (Y, TWO, DOWN_1))),
+            )
+
+    load_dy.wait()
     for n in (THIRD, LAST):
         saving(near_first(LAST), n, drain)
-    load_dy.wait()
 
     @pl.loop(0, T // 256)
     def _(t):
@@ -319,6 +311,11 @@
         wide = wide.astype(f32)
         a1[r, :] = (wide * scale_of(wide)).astype(bf16)
         acc[r, :] = jnp.zeros((256, D), f32)
+
+        @pl.when(t == SECOND)
+        def _():
+            ready_d(TWO, FIRST, far_first(FIRST), DOWN_1)
+
 
     def gu_copies(l, k, j, act):
         act(remote(sg.at[3], rd3.at[k % 2], d_s.at[0], d_r3.at[k % 2], at_p))
@@ -389,15 +386,12 @@
         for n in range(2):
             put(n, gg_hbm.at[0, :, 0:C], drain)
 
-    def arrival(l, k):
-        return near_first(k) if l == ONE else far_between(k, 1 - xx)
-
     def gu_parts(l, k):
-        j = arrival(l, k)
+        j = near_first(k)
         return [p0_hbm.at[l, j], rd2_hbm.at[l, j], rx_hbm.at[l, j]]
 
     def bring_gu(l, k):
-        j = arrival(l, k)
+        j = near_first(k)
         parts = gu_parts(l, k)
         remote(sg.at[2], parts[1], d_s.at[1], d_r2.at[l, j], at_p).wait_recv()
         bring(0, parts[0], start)
@@ -406,7 +400,7 @@
         bring(2, parts[2], start)
 
     def add_gu(l, k):
-        j = arrival(l, k)
+        j = near_first(k)
         add_up(gu_parts(l, k), [gg_hbm.at[l, :, cols(j)], gu_hbm.at[l, :, cols(j)]])
 
     def d_parts(l, half):
@@ -461,71 +455,47 @@
 
     @pl.loop(0, 4)
     def _(k):
-        stage(TWO, k, far_between(k), drain)
-        far = (k == SECOND) | (k == THIRD)
+        stage(TWO, k, far_first(k), drain)
 
         @pl.loop(0, T // TM)
         def _(t):
             backward_2(k, t)
 
-            @pl.when((t == FIRST) & (k > FIRST))
-            def _():
-                gu_across(TWO, k - 1, far_between(k - 1))
-
-            @pl.when((t == FIRST) & ((k == THIRD) | (k == LAST)))
-            def _():
-                d_across(TWO, k // 2 + k % 2 - 1)
-
-            @at(t, FIRST, k, SECOND)
-            def _():
-                near_copy(TWO, 0, drain)
-
-            @at(t, FIRST, k, FIRST)
-            def _():
-                forward_x(TWO, GU_3)
-                forward_y(TWO, DOWN_1)
-
-            @at(t, SECOND, k, FIRST)
-            def _():
-                forward_x(TWO, DOWN_2)
-                forward_y(TWO, GU_3)
-
-            @at(t, THIRD, k, FIRST)
-            def _():
-                forward_x(TWO, GU_4)
-                forward_y(TWO, DOWN_2)
-                landed(TWO, GU_2, DOWN_1)
-                stage(TWO, SECOND, far_between(SECOND), start)
-
-            @at(t, FIRST, k, SECOND)
-            def _():
-                forward_y(TWO, GU_4)
-
-            @at(t, THIRD, k, SECOND)
-            def _():
-                landed(TWO, GU_3, DOWN_2)
-                stage(TWO, THIRD, far_between(THIRD), start)
-
-            @at(t, THIRD, k, THIRD)
-            def _():
-                landed(TWO, GU_4)
-                stage(TWO, LAST, far_between(LAST), start)
-
-            @at(t, THIRD, k, LAST)
-            def _():
-                stage_d(ONE, FIRST, far_first(FIRST), start)
+            def sums():
+                @pl.when(k > FIRST)
+                def _():
+                    gu_across(TWO, k - 1, far_first(k - 1))
+
+                @pl.when((k == SECOND) | (k == THIRD))
+                def _():
+                    d_across(TWO, k - 1)
+
+            duties(
+                t, k,
+                (FIRST, None, sums),
+                (FIRST, FIRST, pass_later((X, TWO, DOWN_2), (Y, TWO, GU_2))),
+                (SECOND, FIRST, pass_later((X, TWO, GU_3), (Y, TWO, DOWN_2))),
+                (THIRD, FIRST, pass_later((X, TWO, GU_4))),
+                (THIRD, FIRST, later(ready, TWO, SECOND, far_first(SECOND), GU_2, DOWN_2)),
+                (LAST, FIRST, pass_later((Y, TWO, GU_3))),
+                (FIRST, SECOND, pass_later((Y, TWO, GU_4))),
+                (THIRD, SECOND, later(ready, TWO, THIRD, far_first(THIRD), GU_3)),
+                (THIRD, THIRD, later(ready, TWO, LAST, far_first(LAST), GU_4)),
+                (FIRST, LAST, later(near_copy, TWO, 0, drain)),
+                (THIRD, LAST, later(stage_d, ONE, FIRST, far_first(FIRST), start)),
+            )
 
         round_gu()
-        round_d(k // 2)
-        gu_copies(TWO, k, far_between(k), start)
-
-        @pl.when(far)
+        round_d(k % 2)
+        gu_copies(TWO, k, far_first(k), start)
+
+        @pl.when(k < THIRD)
         def _():
-            far_copy(k // 2).start()
-
-        @pl.when(jnp.logical_not(far))
+            far_copy(k).start()
+
+        @pl.when(k >= THIRD)
         def _():
-            near_copy(TWO, k // 2, start)
+            near_copy(TWO, k - 2, start)
 
     def product(j, to):
         return pltpu.make_async_copy(act_hbm.at[j], to, ld.at[0])
@@ -543,8 +513,7 @@
         down = (da * scale - wide * mix).astype(bf16)
         do[r, :] = (do[r, :].astype(f32) + down.astype(f32)).astype(bf16)
 
-    gu_across(TWO, LAST, far_between(LAST))
-    near_copy(TWO, 1, drain)
+    gu_across(TWO, LAST, far_first(LAST))
 
     def down_grad(k, of, then, then_of):
         product(far_first(k), of).wait()
@@ -559,6 +528,7 @@
     round_d(0)
     far_copy(0).start()
     down_grad(SECOND, h, THIRD, a1)
+    near_copy(TWO, 1, drain)
     d_across(ONE, 0)
     round_d(1)
     far_copy(1).start()
@@ -579,39 +549,44 @@
         def _(t):
             backward_1(k, t)
 
-            @at(t, FIRST, k, FIRST)
-            def _():
-                near_copy(ONE, 1, drain)
-                other_core_d(TWO)
-
-            @pl.when((t == FIRST) & ((k == SECOND) | (k == THIRD)))
-            def _():
-                add_d(TWO, k - 1)
-
-            @pl.when((t == FIRST) & (k > FIRST))
-            def _():
-                put_done()
-
-            @pl.when(t == FIRST)
-            def _():
+            def fetch():
+                @pl.when(k == FIRST)
+                def _():
+                    near_copy(ONE, 1, drain)
+                    other_core_d(TWO)
+
+                @pl.when((k == SECOND) | (k == THIRD))
+                def _():
+                    add_d(TWO, k - 1)
+
+                @pl.when(k > FIRST)
+                def _():
+                    put_done()
+
                 bring_gu(TWO, k)
 
-            @pl.when((t == SECOND) & (k > FIRST))
-            def _():
-                gu_across(ONE, k - 1, far_first(k - 1))
-
-            @pl.when((t == SECOND) & (k < LAST))
-            def _():
-                stage_d(ONE, k + 1, far_first(k + 1), start)
-
-            @pl.when(t == THIRD)
-            def _():
-                add_gu(TWO, k)
-
-            @pl.when((t == LAST) & (k < THIRD))
-            def _():
-                put_done()
-                bring_d(TWO, k)
+            def sums():
+                @pl.when(k > FIRST)
+                def _():
+                    gu_across(ONE, k - 1, far_first(k - 1))
+
+                @pl.when(k < LAST)
+                def _():
+                    stage_d(ONE, k + 1, far_first(k + 1), start)
+
+            def fetch_d():
+                @pl.when(k < THIRD)
+                def _():
+                    put_done()
+                    bring_d(TWO, k)
+
+            duties(
+                t, k,
+                (FIRST, None, fetch),
+                (SECOND, None, sums),
+                (THIRD, None, later(add_gu, TWO, k)),
+                (LAST, None, fetch_d),
+            )
 
         round_gu()
         gu_copies(ONE, k, far_first(k), start)

time: 305 us -> 297 us (0.974)
  Pallas kernels: 304 us -> 295 us
    pallas_call x1, Pallas kernels: 277 us -> 269 us  [gradients(): pl.pallas_call(step_kernel, in_specs=[hbm] * 5, out_specs=[hbm] * 3 + [vm...]
where the time goes in v4:
time: 297 us; the launch traced here: 296 us
  Pallas kernels  295 us (99%)
    pallas_call x1, Pallas kernels, gradients(): pl.pallas_call(step_kernel, in_specs=[hbm] * 5, out_specs=[hbm] * 3 + [vm...  269 us
    pallas_call x1, Pallas kernels, adamw(): pl.pallas_call(adamw_kernel, grid=(L * N,), in_specs=[pl.BlockSpec((8, 12...  26.4 us

profile of v4, /device:TPU:0, one launch (start us, length us, event | category | flops | bytes accessed | tf_op | source)
XLA Modules:
  0.0 296.3 jit_solution(5883811412973862257)
XLA Ops:
  0.6 269.1 %train_step.1 = (bf16[2,192,3072]{2,1,0:T(8,128)(2,1)}, bf16[2,192,3072]{2,1,0:T(8,128)(2,1)}, bf16[2,768,768]{2,1,0:T(8,128)(2,1)}, f32[8,128]{1,0:T(8,128)}, b...) custom-call(bf16[2048,768]{1,0:T(8,128)(2,1)} %bitcast.2, ...), custom_call_target="tpu_custom_call" | custom-call | tf_op jit(solution)/shard_map/train_step/pallas_call | solution.py:647
  269.7 26.4 %adamw.1 = (bf16[2,192,3072]{2,1,0:T(8,128)(2,1)}, bf16[2,192,3072]{2,1,0:T(8,128)(2,1)}, bf16[2,768,768]{2,1,0:T(8,128)(2,1)}, f32[2,192,3072]{2,1,0:T(8,128)},...) custom-call(f32[8,128]{1,0:T(8,128)} %get-tuple-element.13.refs_0_, ...), custom_call_target="tpu_custom_call" | custom-call | tf_op jit(solution)/shard_map/adamw/pallas_call | solution.py:697

commit v5 on v4

--- a/solution.py
+++ b/solution.py
@@ -14,7 +14,8 @@
 RH = RB // 2
 DH = C // 2
 DQ = C // 4
-N = 4
+ADAMW = 40
+MEGA = 40
 COUNT = 3 * L * D * FF
 FIRST, SECOND, THIRD, LAST = range(4)
 OVER_X, OVER_Y, TO_CORE, Y_TO_CORE = range(4)
@@ -37,10 +38,11 @@
 
 
 def step_kernel(
-    x_hbm, dy_hbm, wg, wu, wd,
+    x_hbm, dy_hbm, wg, wu, wd, m_gate, m_up, m_down,
     gg_hbm, gu_hbm, gd_hbm, fac, all_g, all_u, all_d, p0_hbm, rd2_hbm, rx_hbm, own_d, rd_d, rx_d, up_hbm, act_hbm,
-    h, a0, a1, do, acc, acc_gu, acc_d, w_gu, w_d, act_s, dgu_s, sg, sd, rd3, rd3d, sx, sxd, ssq, ss, ss_src, up_s,
-    ag_s, ag_r, pe_s, pe_r, ld, wsem, d_s, d_r3, dd_s, d_r3d, d_r2, d_rd, keep, x_s, x_r, xd_s, xd_r, fsem, fout, ss_s, ss_r, save, back,
+    acc, acc_gu, up_s, w_gu, w_d,
+    h, a0, a1, do, acc_d, act_s, dgu_s, sg, sd, rd3, rd3d, sx, sxd, ssq, ss, ss_src,
+    ag_s, ag_r, pe_s, pe_r, ld, wsem, d_s, d_r3, dd_s, d_r3d, d_r2, d_rd, keep, x_s, x_r, xd_s, xd_r, fsem, fout, ss_s, ss_r, save, back, early, late,
 ):
     y, i = lax.axis_index("rep"), lax.axis_index("dp")
     xx, c = i // 2, i % 2
@@ -515,6 +517,27 @@
 
     gu_across(TWO, LAST, far_first(LAST))
 
+    def wide_halves(ref, to, sems):
+        for l in range(L):
+            for half in range(2):
+                r = (2 * l + half) * RB
+                yield pltpu.make_async_copy(ref.at[l, :, half * 2 * C : (half + 1) * 2 * C], to(l, half, r), sems.at[2 * l + half])
+
+    def early_loads():
+        for m, ref in enumerate((wg, wu)):
+            yield from wide_halves(ref, lambda l, half, r: w_gu.at[m, r : r + RB, :], early.at[m])
+        for l in range(L):
+            yield pltpu.make_async_copy(m_down.at[l], acc.at[l * C : (l + 1) * C, :], early.at[2, l])
+
+    def late_loads():
+        yield from wide_halves(m_gate, lambda l, half, r: acc_gu.at[r : r + RB, :], late.at[0])
+        yield from wide_halves(m_up, lambda l, half, r: up_s.at[l, half * RB : (half + 1) * RB, :], late.at[1])
+        for l in range(L):
+            yield pltpu.make_async_copy(wd.at[l], w_d.at[l], late.at[2, l])
+
+    for load in early_loads():
+        load.start()
+
     def down_grad(k, of, then, then_of):
         product(far_first(k), of).wait()
         if then is not None:
@@ -591,6 +614,8 @@
         round_gu()
         gu_copies(ONE, k, far_first(k), start)
 
+    for load in late_loads():
+        load.start()
     gu_across(ONE, LAST, far_first(LAST))
     other_core_d(ONE)
 
@@ -634,45 +659,48 @@
     for tell in tells:
         tell.wait_send()
     put_done()
+    for load in (*early_loads(), *late_loads()):
+        load.wait()
     ss[i] = part
     total = jnp.sum(ss[0] + ss[1] + ss[2] + ss[3])
     fac[...] = jnp.minimum(1.0, 0.5 * lax.rsqrt(jnp.full((8, 128), total / COUNT + 1e-30, f32)))
 
 
-def gradients(x, dy, wg, wu, wd):
+def gradients(x, dy, w, m):
     hbm = pl.BlockSpec(memory_space=pl.ANY)
     vmem = pl.BlockSpec(memory_space=pltpu.VMEM)
     out = lambda *shape: jax.ShapeDtypeStruct(shape, bf16)
     dma = lambda *shape: pltpu.SemaphoreType.DMA(shape)
     return pl.pallas_call(
         step_kernel,
-        in_specs=[hbm] * 5,
-        out_specs=[hbm] * 3 + [vmem] + [hbm] * 11,
+        in_specs=[hbm] * 8,
+        out_specs=[hbm] * 3 + [vmem] + [hbm] * 11 + [vmem] * 5,
         out_shape=[
             out(L, RB, FF), out(L, RB, FF), out(L, C, D), jax.ShapeDtypeStruct((8, 128), f32),
             out(L, D, FF), out(L, D, FF), out(L, FF, D),
             out(L, 4, 2 * RB, C), out(L, 4, 2 * RB, C), out(L, 4, 2 * RB, C),
             out(L, C, D), out(L, C, D), out(L, C, D),
             jax.ShapeDtypeStruct((4, T, 2 * C), f32), out(4, T, C),
+            pltpu.VMEM((T, D), f32), pltpu.VMEM((D, 2 * C), f32), pltpu.VMEM((2, TM, 2 * C), f32),
+            pltpu.VMEM((2, D, 2 * C), bf16), pltpu.VMEM((2, C, D), bf16),
         ],
         scratch_shapes=[
             pltpu.VMEM((T, D), bf16), pltpu.VMEM((T, D), bf16), pltpu.VMEM((T, D), bf16), pltpu.VMEM((T, D), bf16),
-            pltpu.VMEM((T, D), f32), pltpu.VMEM((D, 2 * C), f32), pltpu.VMEM((C, D), f32),
-            pltpu.VMEM((2, D, 2 * C), bf16), pltpu.VMEM((2, C, D), bf16),
+            pltpu.VMEM((C, D), f32),
             pltpu.VMEM((TM, C), bf16), pltpu.VMEM((TM, 2 * C), bf16),
             pltpu.VMEM((4, 2 * RB, C), bf16), pltpu.VMEM((2, C, D), bf16),
             pltpu.VMEM((2, 2 * RB, C), bf16), pltpu.VMEM((2, DH, D), bf16),
             pltpu.VMEM((4, 2 * RB, C), bf16), pltpu.VMEM((2, 2, DH, D), bf16),
-            pltpu.VMEM((8, D), f32), pltpu.VMEM((4, 8, 128), f32), pltpu.VMEM((8, 128), f32), pltpu.VMEM((2, TM, 2 * C), f32),
+            pltpu.VMEM((8, D), f32), pltpu.VMEM((4, 8, 128), f32), pltpu.VMEM((8, 128), f32),
             dma(L, 10, 4), dma(L, 10, 4), dma(L, 3), dma(L, 3), dma(2), dma(2, 7),
             dma(2), dma(2), dma(2, 2), dma(2), dma(L, 4), dma(L), dma(2), dma(4), dma(L, 4), dma(L, 2), dma(L, 2),
-            dma(3), dma(2), dma(3), dma(4), dma(2, 2), dma(2),
+            dma(3), dma(2), dma(3), dma(4), dma(2, 2), dma(2), dma(3, 4), dma(3, 4),
         ],
         compiler_params=pltpu.CompilerParams(
-            collective_id=0, has_side_effects=True, vmem_limit_bytes=63 * 2**20
+            collective_id=0, has_side_effects=True, vmem_limit_bytes=MEGA * 2**20
         ),
         name="train_step",
-    )(x, dy, wg, wu, wd)
+    )(x, dy, *w, *m)
 
 
 def adamw_kernel(*refs):
@@ -680,8 +708,9 @@
     factor = fac[0:1, 0:1]
     for n in range(3):
         g, w, m, v = (ins[3 * which + n] for which in range(4))
+        shape = g.shape[1:]
         grad = g[0].astype(f32) * factor
-        new_m = 0.9 * m[0] + 0.1 * grad
+        new_m = 0.9 * m[...].reshape(shape) + 0.1 * grad
         new_v = 0.95 * v[0] + 0.05 * grad * grad
         wide = w[0].astype(f32)
         outs[n][0] = (wide - 0.02 * (new_m * lax.rsqrt(new_v + 1e-8) + 0.1 * wide)).astype(bf16)
@@ -689,27 +718,39 @@
         outs[6 + n][0] = new_v
 
 
-def adamw(factor, g, w, m, v):
-    wide = pl.BlockSpec((1, RB // N, FF), lambda t: (t // N, t % N, 0))
-    tall = pl.BlockSpec((1, C // N, D), lambda t: (t // N, t % N, 0))
-    specs = [wide, wide, tall]
-    shapes = lambda dtype: [jax.ShapeDtypeStruct(a.shape, dtype) for a in w]
+def adamw(factor, g, v, m_down, m_gate, m_up, w_gu, w_d):
+    n = 2
+    rows, tall = RB // n, C // (2 * n)
+    half = (rows, 2 * C)
+    wide = pl.BlockSpec((1, *half), lambda t: (t // (2 * n), t % n, t // n % 2))
+    down = pl.BlockSpec((1, tall, D), lambda t: (t // (2 * n), t % (2 * n), 0))
+    w_at = lambda which: pl.BlockSpec((1, *half), lambda t: (which, t, 0))
+    specs = [wide, wide, down]
+    shapes = lambda dtype: [jax.ShapeDtypeStruct(a.shape, dtype) for a in v]
     return pl.pallas_call(
         adamw_kernel,
-        grid=(L * N,),
-        in_specs=[pl.BlockSpec((8, 128), lambda t: (0, 0))] + specs * 4,
+        grid=(2 * n * L,),
+        in_specs=[pl.BlockSpec((8, 128), lambda t: (0, 0))]
+        + specs
+        + [w_at(0), w_at(1), down]
+        + [
+            pl.BlockSpec(half, lambda t: (t, 0)),
+            pl.BlockSpec((1, *half), lambda t: (t // (2 * n), t % (2 * n), 0)),
+            pl.BlockSpec((tall, D), lambda t: (t, 0)),
+        ]
+        + specs,
         out_specs=specs * 3,
         out_shape=shapes(bf16) + shapes(f32) + shapes(f32),
-        compiler_params=pltpu.CompilerParams(vmem_limit_bytes=63 * 2**20),
+        compiler_params=pltpu.CompilerParams(vmem_limit_bytes=ADAMW * 2**20),
         name="adamw",
-    )(factor, *g, *w, *m, *v)
+    )(factor, *g, *(pltpu.with_memory_space_constraint(a, pltpu.VMEM) for a in (w_gu, w_gu, w_d, m_gate, m_up, m_down)), *v)
 
 
 def solution(mesh):
     def step(x, dy, *arrays):
         w, m, v = (arrays[n : n + 3] for n in (0, 3, 6))
-        gg, gu, gd, factor, *_ = gradients(x[0], dy[0], *w)
-        return tuple(adamw(factor, (gg, gu, gd), w, m, v))
+        gg, gu, gd, factor, *rest = gradients(x[0], dy[0], w, m)
+        return tuple(adamw(factor, (gg, gu, gd), v, *rest[-5:]))
 
     states, cut = P(("rep", "dp"), None, None), P(None, "dp", None)
     return jax.shard_map(

time: 297 us -> 291 us (0.980)
  Pallas kernels: 295 us -> 290 us
    pallas_call x2, Pallas kernels: 295 us -> 290 us  [the longest x1 269 us: gradients(): pl.pallas_call(step_kernel, in_specs=[hbm] * 8, out_specs=[hbm] * 3 + [vm...]
where the time goes in v5:
time: 291 us; the launch traced here: 290 us
  Pallas kernels  290 us (100%)
    pallas_call x1, Pallas kernels, gradients(): pl.pallas_call(step_kernel, in_specs=[hbm] * 8, out_specs=[hbm] * 3 + [vm...  269 us
    pallas_call x1, Pallas kernels, adamw(): pl.pallas_call(adamw_kernel, grid=(2 * n * L,), in_specs=[pl.BlockSpec((8...  20.3 us

profile of v5, /device:TPU:0, one launch (start us, length us, event | category | flops | bytes accessed | tf_op | source)
XLA Modules:
  0.0 290.4 jit_solution(14332092295071526750)
XLA Ops:
  0.6 269.3 %train_step.1 = (bf16[2,192,3072]{2,1,0:T(8,128)(2,1)}, bf16[2,192,3072]{2,1,0:T(8,128)(2,1)}, bf16[2,768,768]{2,1,0:T(8,128)(2,1)}, f32[8,128]{1,0:T(8,128)}, b...) custom-call(bf16[2048,768]{1,0:T(8,128)(2,1)} %bitcast.2, ...), custom_call_target="tpu_custom_call" | custom-call | tf_op jit(solution)/shard_map/train_step/pallas_call | solution.py:674
  270.0 20.3 %adamw.1 = (bf16[2,192,3072]{2,1,0:T(8,128)(2,1)}, bf16[2,192,3072]{2,1,0:T(8,128)(2,1)}, bf16[2,768,768]{2,1,0:T(8,128)(2,1)}, f32[2,192,3072]{2,1,0:T(8,128)},...) custom-call(f32[8,128]{1,0:T(8,128)} %get-tuple-element.18.refs_0_, ...), custom_call_target="tpu_custom_call" | custom-call | tf_op jit(solution)/shard_map/adamw/pallas_call | solution.py:730

commit v6 on v5

--- a/solution.py
+++ b/solution.py
@@ -277,6 +277,10 @@
     def _(k):
         stage(ONE, k, near_first(k), drain)
 
+        @pl.when(k == THIRD)
+        def _():
+            forward_x(ONE, DOWN_2)
+
         @pl.loop(0, T // TM)
         def _(t):
             forward(k, t)
@@ -290,10 +294,9 @@
                 (SECOND, SECOND, later(ready_gu, ONE, THIRD, near_first(THIRD), GU_3)),
                 (THIRD, SECOND, pass_later((X, ONE, GU_4[1:]), (Y, ONE, DOWN_1))),
                 (LAST, SECOND, later(ready_d, ONE, THIRD, near_first(THIRD), DOWN_1)),
-                (FIRST, THIRD, pass_later((X, ONE, DOWN_2), (Y, ONE, GU_4))),
+                (FIRST, THIRD, pass_later((Y, ONE, GU_4))),
                 (SECOND, THIRD, later(ready_gu, ONE, LAST, near_first(LAST), GU_4)),
-                (THIRD, THIRD, pass_later((X, TWO, GU_1[:1]))),
-                (LAST, THIRD, pass_later((X, TWO, GU_1[1:]), (Y, ONE, DOWN_2))),
+                (THIRD, THIRD, pass_later((X, TWO, GU_1), (Y, ONE, DOWN_2))),
                 (LAST, THIRD, later(ready_d, ONE, LAST, near_first(LAST), DOWN_2)),
                 (FIRST, LAST, pass_later((X, TWO, DOWN_1), (Y, TWO, GU_1))),
                 (SECOND, LAST, later(ready_gu, TWO, FIRST, far_first(FIRST), GU_1)),
@@ -314,7 +317,7 @@
         a1[r, :] = (wide * scale_of(wide)).astype(bf16)
         acc[r, :] = jnp.zeros((256, D), f32)
 
-        @pl.when(t == SECOND)
+        @pl.when(t == LAST)
         def _():
             ready_d(TWO, FIRST, far_first(FIRST), DOWN_1)
 
@@ -617,24 +620,6 @@
     for load in late_loads():
         load.start()
     gu_across(ONE, LAST, far_first(LAST))
-    other_core_d(ONE)
-
-    @pl.loop(0, 2)
-    def _(half):
-        put_done()
-        bring_d(ONE, half)
-        add_d(ONE, half)
-
-    @pl.loop(0, 4)
-    def _(k):
-        put_done()
-        bring_gu(ONE, k)
-        add_gu(ONE, k)
-
-    part = ssq[:, :128]
-    for n in range(1, D // 128):
-        part = part + ssq[:, n * 128 : (n + 1) * 128]
-    ss_src[...] = part
     for l in range(L):
         for p in range(10):
             for which, (src, half, to) in enumerate(((ix, y, at_x), (ix, y, at_y), (ix, y, at_p), (ix, 1 - y, at_p))):
@@ -647,6 +632,26 @@
             to_peer(l, m).wait_send()
         for q in range(2):
             xd_copy(l, q).wait_send()
+    for load in (*early_loads(), *late_loads()):
+        load.wait()
+    other_core_d(ONE)
+
+    @pl.loop(0, 2)
+    def _(half):
+        put_done()
+        bring_d(ONE, half)
+        add_d(ONE, half)
+
+    @pl.loop(0, 4)
+    def _(k):
+        put_done()
+        bring_gu(ONE, k)
+        add_gu(ONE, k)
+
+    part = ssq[:, :128]
+    for n in range(1, D // 128):
+        part = part + ssq[:, n * 128 : (n + 1) * 128]
+    ss_src[...] = part
     for k in range(4):
         x_copy(ONE, k, far_first(k)).wait_send()
     tells = [
@@ -659,8 +664,6 @@
     for tell in tells:
         tell.wait_send()
     put_done()
-    for load in (*early_loads(), *late_loads()):
-        load.wait()
     ss[i] = part
     total = jnp.sum(ss[0] + ss[1] + ss[2] + ss[3])
     fac[...] = jnp.minimum(1.0, 0.5 * lax.rsqrt(jnp.full((8, 128), total / COUNT + 1e-30, f32)))

time: 291 us -> 291 us (level)
  no operation moved by 1% of the time
where the time goes in v6:
time: 291 us; the launch traced here: 290 us
  Pallas kernels  289 us (99%)
    pallas_call x1, Pallas kernels, gradients(): pl.pallas_call(step_kernel, in_specs=[hbm] * 8, out_specs=[hbm] * 3 + [vm...  269 us
    pallas_call x1, Pallas kernels, adamw(): pl.pallas_call(adamw_kernel, grid=(2 * n * L,), in_specs=[pl.BlockSpec((8...  20.3 us

profile of v6, /device:TPU:0, one launch (start us, length us, event | category | flops | bytes accessed | tf_op | source)
XLA Modules:
  0.0 289.9 jit_solution(17259178134496146324)
XLA Ops:
  0.6 268.8 %train_step.1 = (bf16[2,192,3072]{2,1,0:T(8,128)(2,1)}, bf16[2,192,3072]{2,1,0:T(8,128)(2,1)}, bf16[2,768,768]{2,1,0:T(8,128)(2,1)}, f32[8,128]{1,0:T(8,128)}, b...) custom-call(bf16[2048,768]{1,0:T(8,128)(2,1)} %bitcast.2, ...), custom_call_target="tpu_custom_call" | custom-call | tf_op jit(solution)/shard_map/train_step/pallas_call | solution.py:677
  269.4 20.3 %adamw.1 = (bf16[2,192,3072]{2,1,0:T(8,128)(2,1)}, bf16[2,192,3072]{2,1,0:T(8,128)(2,1)}, bf16[2,768,768]{2,1,0:T(8,128)(2,1)}, f32[2,192,3072]{2,1,0:T(8,128)},...) custom-call(f32[8,128]{1,0:T(8,128)} %get-tuple-element.18.refs_0_, ...), custom_call_target="tpu_custom_call" | custom-call | tf_op jit(solution)/shard_map/adamw/pallas_call | solution.py:733
